TPU v7x, 32 devices: a whole 2x2x4 slice. The times are simulated.
32 devices in a mesh: tm: 8 (over z, x), space: 4 (over y, core).
Axes of the slice: x: 2, y: 2, z: 4, core: 2. Of those that a mesh axis runs over, the one named last changes fastest.
Arguments:
- u_old: float32 [8, 5, 256, 16, 128], P('tm', None, 'space'), may hold values from -2.5 to 2.5
- u_init: float32 [256, 16, 128], P('space'), may hold values from -2.5 to 2.5
Outputs:
- u_new: float32 [8, 5, 256, 16, 128], P('tm', None, 'space')
All inputs are finite; a program needn't handle non-finite values.
Results may differ from a plain program's by a relative error of at most 0.0003.
Values sent between devices are 32-bit elements; how exact they have to be, the bound alone decides.
A program may use at most 128 MiB of HBM per device.

v0:
```python
import functools
import math

import jax
import jax.numpy as jnp
import numpy as np
from jax import lax
from jax.experimental import pallas as pl
from jax.experimental.pallas import tpu as pltpu
from jax.sharding import PartitionSpec as P

step_length = 0.4
diffusion = 1.0
reaction = 1.0
HALO = 5
BLOCK = 4
MESH = pl.DeviceIdType.MESH


def basis_coefficients(nodes, chosen):
    polynomial = [1.0]
    for other, point in enumerate(nodes):
        if other == chosen:
            continue
        divisor = nodes[chosen] - point
        widened = [0.0] * (len(polynomial) + 1)
        for power, value in enumerate(polynomial):
            widened[power + 1] += value / divisor
            widened[power] -= value * point / divisor
        polynomial = widened
    return polynomial


def basis_value(nodes, chosen, where):
    result = 1.0
    for other, point in enumerate(nodes):
        if other != chosen:
            result *= (where - point) / (nodes[chosen] - point)
    return result


def node_tables():
    root = math.sqrt(3.0 / 7.0)
    fine_tau = [0.0, (1.0 - root) / 2.0, 0.5, (1.0 + root) / 2.0, 1.0]
    coarse_tau = [0.0, 0.5, 1.0]
    integ = []
    for j in range(4):
        row_values = []
        for k in range(5):
            polynomial = basis_coefficients(fine_tau, k)
            total = 0.0
            for power, value in enumerate(polynomial):
                total += (
                    value
                    * (fine_tau[j + 1] ** (power + 1) - fine_tau[j] ** (power + 1))
                    / (power + 1)
                )
            row_values.append(total)
        integ.append(row_values)
    interp = [[basis_value(coarse_tau, c, fine_tau[m]) for c in range(3)] for m in range(5)]
    spacing = [float(fine_tau[j + 1] - fine_tau[j]) for j in range(4)]
    return integ, spacing, interp


def hartley(length):
    counter = np.arange(length)
    phase = 2.0 * np.pi * (counter[:, None] * counter[None, :] % length) / length
    return (np.cos(phase) + np.sin(phase)) / math.sqrt(length)


def two_parts(table):
    upper = table.astype(jnp.bfloat16)
    lower = (table - upper.astype(np.float64)).astype(jnp.bfloat16)
    return np.stack([upper, lower])


def halves(value):
    upper = value.astype(jnp.bfloat16)
    return upper, (value - upper.astype(jnp.float32)).astype(jnp.bfloat16)


def product(a, b, dims):
    def one(x, y):
        return lax.dot_general(x, y, (dims, ((), ())), preferred_element_type=jnp.float32)

    return one(a[0], b[0]) + (one(a[0], b[1]) + one(a[1], b[0]))


def force(padded):
    field = padded[1:-1]
    rows, cols = field.shape[1:]
    near = padded[2:] + padded[:-2]
    near = near + (pltpu.roll(field, 1, 1) + pltpu.roll(field, rows - 1, 1))
    near = near + (pltpu.roll(field, 1, 2) + pltpu.roll(field, cols - 1, 2))
    linear = reaction - 6.0 * diffusion
    return diffusion * near + field * (linear - reaction * (field * field))


def kernel(
    nt, ns, solvers,
    u_hbm, init_hbm, tab_hbm, ztab_hbm, inv_hbm,
    out,
    u, w, corr, acc, restricted, tab, ztab, inv,
    send_1, recv_1, send_2, recv_2, up,
    load_sem, table_sem, start_sem, halo_send, halo_recv, start_send, start_recv,
    sems, known_sem,
):
    integ, spacing, interp = node_tables()
    h = step_length
    devices = nt * ns
    depth, rows, cols = init_hbm.shape
    depth_c, rows_c = depth // 2, rows // 2
    length = send_1.shape[2]
    modes = send_1.shape[1]
    own = pl.ds(HALO, depth)
    t, s = lax.axis_index("tm"), lax.axis_index("space")
    me = t * ns + s
    above, below = lax.rem(s + 1, ns), lax.rem(s + ns - 1, ns)

    barrier = pltpu.get_barrier_semaphore()

    def signal_along(sem, step):
        @pl.when(t + step < nt)
        def _():
            pl.semaphore_signal(sem, inc=1, device_id=(t + step, s), device_id_type=MESH)

        @pl.when(t >= step)
        def _():
            pl.semaphore_signal(sem, inc=1, device_id=(t - step, s), device_id_type=MESH)

    def sides(step):
        return jnp.where(t + step < nt, 1, 0) + jnp.where(t >= step, 1, 0)

    signal_along(barrier, 1)
    for i in range(1, ns):
        pl.semaphore_signal(
            barrier, inc=1, device_id=(t, lax.rem(s + i, ns)), device_id_type=MESH
        )
    load = pltpu.make_async_copy(u_hbm.at[0], u.at[:, own], load_sem)
    load.start()
    tables = [
        pltpu.make_async_copy(source, target, table_sem.at[i])
        for i, (source, target) in enumerate(((tab_hbm, tab), (ztab_hbm, ztab), (inv_hbm, inv)))
    ]
    for copy in tables:
        copy.start()
    local_start = pltpu.make_async_copy(init_hbm, w.at[0, own], start_sem)

    @pl.when(t == 0)
    def _():
        local_start.start()

    pl.semaphore_wait(barrier, ns - 1 + sides(1))

    lows, highs = pl.ds(0, HALO), pl.ds(HALO + depth, HALO)
    first, last = pl.ds(0, HALO), pl.ds(depth - HALO, HALO)

    def remote(source, target, send, recv, place):
        return pltpu.make_async_remote_copy(
            src_ref=source, dst_ref=target, send_sem=send, recv_sem=recv,
            device_id=place, device_id_type=MESH,
        )

    after = jnp.minimum(t + 1, nt - 1)
    node = u_hbm.at[0, 4]
    cuts = [(0, HALO), (depth - HALO, HALO), (HALO, depth - 2 * HALO)]
    starts = [
        remote(
            node.at[pl.ds(begin, size)], w.at[0, pl.ds(HALO + begin, size)],
            start_send.at[i], start_recv.at[i], (after, s),
        )
        for i, (begin, size) in enumerate(cuts)
    ]

    def edges(source, shift):
        return [
            remote(
                source.at[pl.ds(shift + depth - HALO, HALO)], w.at[0, lows],
                start_send.at[3], start_recv.at[3], (t, above),
            ),
            remote(
                source.at[pl.ds(shift, HALO)], w.at[0, highs],
                start_send.at[4], start_recv.at[4], (t, below),
            ),
        ]

    inits, passed = edges(init_hbm, 0), edges(w.at[0], HALO)
    halos = [
        remote(u_hbm.at[0, :, last], u.at[:, lows], halo_send.at[0], halo_recv.at[0], (t, above)),
        remote(u_hbm.at[0, :, first], u.at[:, highs], halo_send.at[1], halo_recv.at[1], (t, below)),
    ]
    @pl.when(t < nt - 1)
    def _():
        for copy in starts:
            copy.start()

    for copy in halos:
        copy.start()

    @pl.when(t == 0)
    def _():
        for copy in inits:
            copy.start()

    signal_along(known_sem.at[0], 1)
    load.wait()
    for copy in halos:
        copy.wait_recv()

    blocks = (depth + 2 * HALO - 2) // BLOCK

    def fold_block(i, carry):
        z = 1 + i * BLOCK
        forces = [force(u[k, pl.ds(z - 1, BLOCK + 2)]) for k in range(5)]
        for j in range(4):
            total = None
            for k in range(5):
                weight = h * integ[j][k] - (h * spacing[j] if j == k else 0.0)
                term = weight * forces[k]
                total = term if total is None else total + term
            corr[j, pl.ds(z, BLOCK)] = total
        return carry

    lax.fori_loop(0, blocks, fold_block, 0)

    @pl.when(t == 0)
    def _():
        local_start.wait()

    @pl.when(t > 0)
    def _():
        starts[1].wait_recv()
        passed[0].start()
        starts[0].wait_recv()
        passed[1].start()

    for i in range(known_sem.shape[0]):
        if i > 0:
            signal_along(known_sem.at[i], 2 ** i)
        pl.semaphore_wait(known_sem.at[i], sides(2 ** i))

    @pl.when(t > 0)
    def _():
        starts[2].wait_recv()

    for copy in inits:
        copy.wait_recv()

    for m in range(4):
        def sweep_block(i, carry, m=m):
            z = 1 + i * BLOCK
            here = pl.ds(z, BLOCK)
            padded = w[m, pl.ds(z - 1, BLOCK + 2)]
            now = force(padded)
            w[m + 1, here] = padded[1:-1] + (h * spacing[m]) * now + corr[m, here]
            for a in range(2):
                term = (h * (integ[2 * a][m] + integ[2 * a + 1][m])) * now
                acc[a, here] = term if m == 0 else acc[a, here] + term
            return carry

        lax.fori_loop(0, blocks, sweep_block, 0)

    plane = rows * depth_c

    def last_block(i, carry):
        z = HALO + i * BLOCK
        here = pl.ds(z, BLOCK)
        padded = w[4, pl.ds(z - 1, BLOCK + 2)]
        now, end = force(padded), padded[1:-1]
        middle = w[2, here]
        outs = []
        for a in range(2):
            term = acc[a, here] + (h * (integ[2 * a][4] + integ[2 * a + 1][4])) * now
            outs.append(term + ((w[0, here] - middle) if a == 0 else (middle - end)))
        outs.append(end - u[4, here])
        for f in range(3):
            pair = outs[f].reshape(BLOCK // 2, 2, rows, cols)
            pair = pair[:, 0] + pair[:, 1]
            place = pl.multiple_of(f * plane + i * (BLOCK // 2) * rows, 8)
            restricted[pl.ds(place, BLOCK // 2 * rows), :] = pair.reshape(BLOCK // 2 * rows, cols)
        return carry

    lax.fori_loop(0, depth // BLOCK, last_block, 0)

    filled = 3 * depth_c
    pieces = []
    for x in range(rows_c):
        even = restricted[pl.ds(2 * x, filled, stride=rows), :]
        odd = restricted[pl.ds(2 * x + 1, filled, stride=rows), :]
        pieces.append((even + odd) * 0.125)
    flat = jnp.concatenate(pieces, axis=1)
    if length > filled:
        flat = jnp.concatenate([flat, jnp.zeros((length - filled, rows_c * cols), jnp.float32)], axis=0)
    for copy in tables:
        copy.wait()
    spectral = product((tab[0], tab[1]), halves(flat), ((1,), (1,)))
    send_1[...] = spectral.reshape(solvers, modes, length)

    slot = s * nt + t

    def spread(i, carry):
        other = lax.rem(me + i, solvers)

        @pl.when(other != me)
        def _():
            remote(
                send_1.at[other], recv_1.at[slot], sems.at[0], sems.at[1],
                (other // ns, lax.rem(other, ns)),
            ).start()

        return carry

    lax.fori_loop(0, solvers, spread, 0)

    def when_all(condition, body):
        if solvers == devices:
            body()
        else:
            pl.when(condition)(body)

    def bytes_wait(ref, count, sem):
        part = ref.at[pl.ds(0, count)]
        pltpu.make_async_copy(part, part, sem).wait()

    def solve():
        recv_1[slot] = send_1[me]
        bytes_wait(recv_1, devices - 1, sems.at[1])
        joined = jnp.concatenate(
            [recv_1[pl.ds(q * nt, nt)].reshape(nt * modes, length) for q in range(ns)], axis=1
        )
        spectra = product(halves(joined), (ztab[0], ztab[1]), ((1,), (0,)))
        width = inv.shape[1]
        factor = inv[pl.ds(pl.multiple_of(me * modes, 8), modes), :]
        begin = jnp.zeros((modes, width), jnp.float32)
        rows_of = []
        for n in range(nt):
            part = spectra[n * modes:(n + 1) * modes]
            middle = (begin + part[:, :width]) * factor
            finish = (middle + part[:, width:2 * width]) * factor
            rows_of.append(jnp.concatenate([begin, middle, finish], axis=1))
            begin = finish + part[:, 2 * width:]
        solved = jnp.concatenate(rows_of, axis=0)
        back = product(halves(solved), (ztab[0], ztab[1]), ((1,), (1,)))
        for q in range(ns):
            send_2[pl.ds(q * nt, nt)] = back[:, q * length:(q + 1) * length].reshape(nt, modes, length)

        def give(i, carry):
            other = lax.rem(me + i, devices)
            to_t, to_s = other // ns, lax.rem(other, ns)
            remote(
                send_2.at[to_s * nt + to_t], recv_2.at[me], sems.at[2], sems.at[3], (to_t, to_s)
            ).start()
            return carry

        lax.fori_loop(1, devices, give, 0)
        recv_2[me] = send_2[slot]
        bytes_wait(recv_2, solvers - 1, sems.at[3])

    when_all(me < solvers, solve)
    if solvers != devices:
        @pl.when(me >= solvers)
        def _():
            bytes_wait(recv_2, solvers, sems.at[3])

    delta = jnp.transpose(recv_2[...].reshape(solvers * modes, length))[:filled]
    coarse = product(halves(delta), (tab[0], tab[1]), ((1,), (0,)))
    for x in range(rows_c):
        part = coarse[:, x * cols:(x + 1) * cols]
        for side in range(2):
            up[pl.ds(2 * x + side, filled, stride=rows), :] = part

    def add_block(i, carry):
        fields = [
            up[pl.ds(pl.multiple_of(c * plane + i * (BLOCK // 2) * rows, 8), BLOCK // 2 * rows), :]
            for c in range(3)
        ]
        for m in range(5):
            total = None
            for c in range(3):
                if abs(interp[m][c]) < 1e-14:
                    continue
                term = fields[c]
                if abs(interp[m][c] - 1.0) > 1e-14:
                    term = interp[m][c] * term
                total = term if total is None else total + term
            total = total.reshape(BLOCK // 2, 1, rows, cols)
            total = jnp.broadcast_to(total, (BLOCK // 2, 2, rows, cols)).reshape(BLOCK, rows, cols)
            z = i * BLOCK
            out[0, m, pl.ds(z, BLOCK)] = w[m, pl.ds(HALO + z, BLOCK)] + total
        return carry

    lax.fori_loop(0, depth // BLOCK, add_block, 0)

    for copy in halos:
        copy.wait_send()

    @pl.when(t < nt - 1)
    def _():
        for copy in starts:
            copy.wait_send()

    for copy in inits:
        copy.wait_send()

    def sent():
        bytes_wait(send_1, solvers - 1, sems.at[0])
        bytes_wait(send_2, devices - 1, sems.at[2])

    when_all(me < solvers, sent)
    if solvers != devices:
        @pl.when(me >= solvers)
        def _():
            bytes_wait(send_1, solvers, sems.at[0])


def shards(nt, ns, u_old, u_init):
    depth, rows, cols = u_init.shape
    depth_c, rows_c, cols_c = depth // 2, rows // 2, cols // 2
    whole_c = depth_c * ns
    count = rows_c * cols_c
    devices = nt * ns
    solvers = min(devices, count // 8)
    modes = count // solvers
    length = -(-3 * depth_c // 128) * 128
    extended = depth + 2 * HALO
    rounds = max(1, (nt - 1).bit_length())

    wide = np.repeat(hartley(cols_c), 2, axis=1)
    tab = two_parts(np.kron(hartley(rows_c), wide))
    wave = hartley(whole_c)
    ztab = np.zeros((ns, length, 3 * whole_c))
    for f in range(3):
        ztab[:, f * depth_c:(f + 1) * depth_c, f * whole_c:(f + 1) * whole_c] = wave.reshape(ns, depth_c, whole_c)
    ztab = two_parts(ztab.reshape(ns * length, 3 * whole_c))
    angle_z = 2.0 * np.cos(2.0 * np.pi * np.arange(whole_c) / whole_c)
    angle_x = 2.0 * np.cos(2.0 * np.pi * np.arange(rows_c) / rows_c)
    angle_y = 2.0 * np.cos(2.0 * np.pi * np.arange(cols_c) / cols_c)
    planar = (angle_x[:, None] + angle_y[None, :]).reshape(count)
    eigen = 0.25 * (planar[:, None] + angle_z[None, :] - 6.0)
    inv = (1.0 / (1.0 - 0.5 * step_length * diffusion * eigen)).astype(np.float32)

    f32 = jnp.float32
    return pl.pallas_call(
        functools.partial(kernel, nt, ns, solvers),
        out_shape=jax.ShapeDtypeStruct((1, 5, depth, rows, cols), f32),
        in_specs=[pl.BlockSpec(memory_space=pltpu.HBM)] * 5,
        out_specs=pl.BlockSpec(memory_space=pltpu.VMEM),
        scratch_shapes=[
            pltpu.VMEM((5, extended, rows, cols), f32),
            pltpu.VMEM((5, extended, rows, cols), f32),
            pltpu.VMEM((4, extended, rows, cols), f32),
            pltpu.VMEM((2, extended, rows, cols), f32),
            pltpu.VMEM((3 * depth_c * rows, cols), f32),
            pltpu.VMEM(tab.shape, jnp.bfloat16),
            pltpu.VMEM(ztab.shape, jnp.bfloat16),
            pltpu.VMEM(inv.shape, f32),
            pltpu.VMEM((solvers, modes, length), f32),
            pltpu.VMEM((devices, modes, length), f32),
            pltpu.VMEM((devices, modes, length), f32),
            pltpu.VMEM((solvers, modes, length), f32),
            pltpu.VMEM((3 * depth_c * rows, cols), f32),
            pltpu.SemaphoreType.DMA,
            pltpu.SemaphoreType.DMA((3,)),
            pltpu.SemaphoreType.DMA,
            pltpu.SemaphoreType.DMA((2,)),
            pltpu.SemaphoreType.DMA((2,)),
            pltpu.SemaphoreType.DMA((5,)),
            pltpu.SemaphoreType.DMA((5,)),
            pltpu.SemaphoreType.DMA((4,)),
            pltpu.SemaphoreType.REGULAR((rounds,)),
        ],
        compiler_params=pltpu.CompilerParams(
            collective_id=0, has_side_effects=True, vmem_limit_bytes=62000000
        ),
    )(u_old, u_init, tab, ztab, inv)


def solution(mesh):
    return jax.shard_map(
        functools.partial(shards, mesh.shape["tm"], mesh.shape["space"]),
        mesh=mesh,
        in_specs=(P("tm", None, "space", None, None), P("space", None, None)),
        out_specs=P("tm", None, "space", None, None),
        check_vma=False,
    )
```

profile of v0, /device:TPU:25, one launch (start us, length us, event | category | flops | bytes accessed | tf_op | source)
XLA Modules:
  0.0 49.3 jit_solution(7509000753272284518)
XLA Ops:
  0.0 45.8 %shard_map.55 = f32[1,5,64,16,128]{4,3,2,1,0:T(8,128)} custom-call(f32[1,5,64,16,128]{4,3,2,1,0:T(8,128)} %u_hbm.1, f32[64,16,128]{2,1,0:T(8,128)} %init_hbm.1, bf16[2,512,1024]{2,1,0:T(8,128)(2,1)} %constant.6.clone.tab_hbm, bf16[2,512,384]{2,1,0:T(8,128)(2,1)} %constant.7.clone.ztab_hbm, f32[512,128]{1,0:T(8,128)} %constant.8.clone.inv_hbm), custom_call_target="tpu_custom_call" | custom-call | tf_op jit(solution)/shard_map/pallas_call | solution.py:443
  45.8 3.5 %copy.7 = f32[1,5,64,16,128]{4,3,2,1,0:T(8,128)} copy(f32[1,5,64,16,128]{4,3,2,1,0:T(8,128)} %shard_map.55) | data formatting | bytes 5242880
where the time goes:
time: 49.5 us; the launch traced here: 49.3 us
  Pallas kernels  45.8 us (93%)
  local copies, waits for them, and re-layouts  3.52 us (7%)
    pallas_call x1, Pallas kernels, shards(): pl.pallas_call(functools.partial(kernel, nt, ns, solvers), out_shape=jax....  45.8 us
    unnamed x1, local copies, waits for them, and re-layouts  3.52 us

commit v1 on v0

--- a/solution.py
+++ b/solution.py
@@ -14,6 +14,7 @@
 reaction = 1.0
 HALO = 5
 BLOCK = 4
+PARTS = 4
 MESH = pl.DeviceIdType.MESH
 
 
@@ -99,9 +100,9 @@
 def kernel(
     nt, ns, solvers,
     u_hbm, init_hbm, tab_hbm, ztab_hbm, inv_hbm,
-    out,
-    u, w, corr, acc, restricted, tab, ztab, inv,
-    send_1, recv_1, send_2, recv_2, up,
+    w, up,
+    u, corr, acc, restricted, tab, ztab, inv,
+    send_1, recv_1, send_2, recv_2,
     load_sem, table_sem, start_sem, halo_send, halo_recv, start_send, start_recv,
     sems, known_sem,
 ):
@@ -369,28 +370,6 @@
         for side in range(2):
             up[pl.ds(2 * x + side, filled, stride=rows), :] = part
 
-    def add_block(i, carry):
-        fields = [
-            up[pl.ds(pl.multiple_of(c * plane + i * (BLOCK // 2) * rows, 8), BLOCK // 2 * rows), :]
-            for c in range(3)
-        ]
-        for m in range(5):
-            total = None
-            for c in range(3):
-                if abs(interp[m][c]) < 1e-14:
-                    continue
-                term = fields[c]
-                if abs(interp[m][c] - 1.0) > 1e-14:
-                    term = interp[m][c] * term
-                total = term if total is None else total + term
-            total = total.reshape(BLOCK // 2, 1, rows, cols)
-            total = jnp.broadcast_to(total, (BLOCK // 2, 2, rows, cols)).reshape(BLOCK, rows, cols)
-            z = i * BLOCK
-            out[0, m, pl.ds(z, BLOCK)] = w[m, pl.ds(HALO + z, BLOCK)] + total
-        return carry
-
-    lax.fori_loop(0, depth // BLOCK, add_block, 0)
-
     for copy in halos:
         copy.wait_send()
 
@@ -411,6 +390,42 @@
         @pl.when(me >= solvers)
         def _():
             bytes_wait(send_1, solvers, sems.at[0])
+
+
+def finish(w, up, out, staged, sems):
+    _, _, interp = node_tables()
+    depth, rows, cols = out.shape[2:]
+    plane = rows * (depth // 2)
+    part = depth // PARTS
+
+    def give(p):
+        return pltpu.make_async_copy(staged.at[p], out.at[0, :, pl.ds(p * part, part)], sems.at[p])
+
+    for p in range(PARTS):
+        def add_block(i, carry, p=p):
+            begin = p * part + i * BLOCK
+            count = BLOCK // 2 * rows
+            fields = [
+                up[pl.ds(pl.multiple_of(c * plane + begin // 2 * rows, 8), count), :] for c in range(3)
+            ]
+            for m in range(5):
+                total = None
+                for c in range(3):
+                    if abs(interp[m][c]) < 1e-14:
+                        continue
+                    term = fields[c]
+                    if abs(interp[m][c] - 1.0) > 1e-14:
+                        term = interp[m][c] * term
+                    total = term if total is None else total + term
+                total = total.reshape(BLOCK // 2, 1, rows, cols)
+                total = jnp.broadcast_to(total, (BLOCK // 2, 2, rows, cols)).reshape(BLOCK, rows, cols)
+                staged[p, m, pl.ds(i * BLOCK, BLOCK)] = w[m, pl.ds(HALO + begin, BLOCK)] + total
+            return carry
+
+        lax.fori_loop(0, part // BLOCK, add_block, 0)
+        give(p).start()
+    for p in range(PARTS):
+        give(p).wait()
 
 
 def shards(nt, ns, u_old, u_init):
@@ -440,13 +455,15 @@
     inv = (1.0 / (1.0 - 0.5 * step_length * diffusion * eigen)).astype(np.float32)
 
     f32 = jnp.float32
-    return pl.pallas_call(
+    states, corrections = pl.pallas_call(
         functools.partial(kernel, nt, ns, solvers),
-        out_shape=jax.ShapeDtypeStruct((1, 5, depth, rows, cols), f32),
+        out_shape=(
+            jax.ShapeDtypeStruct((5, extended, rows, cols), f32),
+            jax.ShapeDtypeStruct((3 * depth_c * rows, cols), f32),
+        ),
         in_specs=[pl.BlockSpec(memory_space=pltpu.HBM)] * 5,
-        out_specs=pl.BlockSpec(memory_space=pltpu.VMEM),
+        out_specs=(pl.BlockSpec(memory_space=pltpu.VMEM),) * 2,
         scratch_shapes=[
-            pltpu.VMEM((5, extended, rows, cols), f32),
             pltpu.VMEM((5, extended, rows, cols), f32),
             pltpu.VMEM((4, extended, rows, cols), f32),
             pltpu.VMEM((2, extended, rows, cols), f32),
@@ -458,7 +475,6 @@
             pltpu.VMEM((devices, modes, length), f32),
             pltpu.VMEM((devices, modes, length), f32),
             pltpu.VMEM((solvers, modes, length), f32),
-            pltpu.VMEM((3 * depth_c * rows, cols), f32),
             pltpu.SemaphoreType.DMA,
             pltpu.SemaphoreType.DMA((3,)),
             pltpu.SemaphoreType.DMA,
@@ -470,9 +486,20 @@
             pltpu.SemaphoreType.REGULAR((rounds,)),
         ],
         compiler_params=pltpu.CompilerParams(
-            collective_id=0, has_side_effects=True, vmem_limit_bytes=62000000
+            collective_id=0, has_side_effects=True, vmem_limit_bytes=30000000
         ),
-    )(u_old, u_init, tab, ztab, inv)
+    )(*(pltpu.with_memory_space_constraint(a, pltpu.HBM) for a in (u_old, u_init, tab, ztab, inv)))
+    return pl.pallas_call(
+        finish,
+        out_shape=jax.ShapeDtypeStruct((1, 5, depth, rows, cols), f32),
+        in_specs=[pl.BlockSpec(memory_space=pltpu.VMEM)] * 2,
+        out_specs=pl.BlockSpec(memory_space=pltpu.HBM),
+        scratch_shapes=[
+            pltpu.VMEM((PARTS, 5, depth // PARTS, rows, cols), f32),
+            pltpu.SemaphoreType.DMA((PARTS,)),
+        ],
+        compiler_params=pltpu.CompilerParams(vmem_limit_bytes=16000000),
+    )(states, corrections)
 
 
 def solution(mesh):

time: 49.5 us -> 45.8 us (0.925)
  local copies, waits for them, and re-layouts: 3.52 us -> 0 us
    unnamed x1 -> x0, local copies, waits for them, and re-layouts: 3.52 us -> none
    pallas_call x1 -> x2, Pallas kernels: 45.8 us -> 45.6 us  [the longest x1 44 us: shards(): pl.pallas_call(functools.partial(kernel, nt, ns, solvers), out_shape=(jax...]
where the time goes in v1:
time: 45.8 us; the launch traced here: 45.6 us
  Pallas kernels  45.6 us (100%)
    pallas_call x1, Pallas kernels, shards(): pl.pallas_call(functools.partial(kernel, nt, ns, solvers), out_shape=(jax...  44 us
    pallas_call x1, Pallas kernels, shards(): pl.pallas_call(finish, out_shape=jax.ShapeDtypeStruct((1, 5, depth, rows,...  1.61 us

profile of v1, /device:TPU:25, one launch (start us, length us, event | category | flops | bytes accessed | tf_op | source)
XLA Modules:
  0.0 45.6 jit_solution(10492774004931422323)
XLA Ops:
  0.0 44.0 %shard_map.55 = (f32[5,74,16,128]{3,2,1,0:T(8,128)S(1)}, f32[1536,128]{1,0:T(8,128)S(1)}) custom-call(f32[1,5,64,16,128]{4,3,2,1,0:T(8,128)} %u_hbm.1, f32[64,16,128]{2,1,0:T(8,128)} %init_hbm.1, bf16[2,512,1024]{2,1,0:T(8,128)(2,1)} %constant.6.clone.tab_hbm, bf16[2,512,384]{2,1,0:T(8,128)(2,1)} %constant.7.clone.ztab_hbm, f32[512,128]{1,0:T(8,128)} %constant.8.clone.inv_hbm), custom_call_target="tpu_custom_call" | custom-call | tf_op jit(solution)/shard_map/pallas_call | solution.py:458
  44.0 1.6 %shard_map.56 = f32[1,5,64,16,128]{4,3,2,1,0:T(8,128)} custom-call(f32[5,74,16,128]{3,2,1,0:T(8,128)S(1)} %get-tuple-element.7.w, f32[1536,128]{1,0:T(8,128)S(1)} %get-tuple-element.8.up), custom_call_target="tpu_custom_call" | custom-call | tf_op jit(solution)/shard_map/pallas_call | solution.py:492

commit v2 on v1

v2 whole, which is shorter than its diff:
```python
import functools
import math

import jax
import jax.numpy as jnp
import numpy as np
from jax import lax
from jax.experimental import pallas as pl
from jax.experimental.pallas import tpu as pltpu
from jax.sharding import PartitionSpec as P

step_length = 0.4
diffusion = 1.0
reaction = 1.0
HALO = 5
BLOCK = 8
PIECE = 4
PARTS = 4
GROUPS = 2
MESH = pl.DeviceIdType.MESH


def basis_coefficients(nodes, chosen):
    polynomial = [1.0]
    for other, point in enumerate(nodes):
        if other == chosen:
            continue
        divisor = nodes[chosen] - point
        widened = [0.0] * (len(polynomial) + 1)
        for power, value in enumerate(polynomial):
            widened[power + 1] += value / divisor
            widened[power] -= value * point / divisor
        polynomial = widened
    return polynomial


def basis_value(nodes, chosen, where):
    result = 1.0
    for other, point in enumerate(nodes):
        if other != chosen:
            result *= (where - point) / (nodes[chosen] - point)
    return result


def node_tables():
    root = math.sqrt(3.0 / 7.0)
    fine_tau = [0.0, (1.0 - root) / 2.0, 0.5, (1.0 + root) / 2.0, 1.0]
    coarse_tau = [0.0, 0.5, 1.0]
    integ = []
    for j in range(4):
        row_values = []
        for k in range(5):
            polynomial = basis_coefficients(fine_tau, k)
            total = 0.0
            for power, value in enumerate(polynomial):
                total += (
                    value
                    * (fine_tau[j + 1] ** (power + 1) - fine_tau[j] ** (power + 1))
                    / (power + 1)
                )
            row_values.append(total)
        integ.append(row_values)
    interp = [[basis_value(coarse_tau, c, fine_tau[m]) for c in range(3)] for m in range(5)]
    spacing = [float(fine_tau[j + 1] - fine_tau[j]) for j in range(4)]
    return integ, spacing, interp


def hartley(length):
    counter = np.arange(length)
    phase = 2.0 * np.pi * (counter[:, None] * counter[None, :] % length) / length
    return (np.cos(phase) + np.sin(phase)) / math.sqrt(length)


def two_parts(table):
    upper = table.astype(jnp.bfloat16)
    lower = (table - upper.astype(np.float64)).astype(jnp.bfloat16)
    return np.stack([upper, lower])


def halves(value):
    upper = value.astype(jnp.bfloat16)
    return upper, (value - upper.astype(jnp.float32)).astype(jnp.bfloat16)


def product(a, b, dims):
    def one(x, y):
        return lax.dot_general(x, y, (dims, ((), ())), preferred_element_type=jnp.float32)

    return one(a[0], b[0]) + (one(a[0], b[1]) + one(a[1], b[0]))


def force(padded):
    field = padded[1:-1]
    rows, cols = field.shape[1:]
    near = padded[2:] + padded[:-2]
    near = near + (pltpu.roll(field, 1, 1) + pltpu.roll(field, rows - 1, 1))
    near = near + (pltpu.roll(field, 1, 2) + pltpu.roll(field, cols - 1, 2))
    linear = reaction - 6.0 * diffusion
    return diffusion * near + field * (linear - reaction * (field * field))


def kernel(
    nt, ns, groups,
    u_hbm, init_hbm, ytab_hbm, xtab_hbm, ztab_hbm, inv_hbm,
    w, up,
    u, corr, forces, restricted, ytab, ytab_back, xtab, ztab, inv,
    send_1, recv_1, send_2, recv_2, carry_out, carry_in,
    load_sem, table_sem, start_sem, halo_send, halo_recv, start_send, start_recv,
    sems, known_sem,
):
    integ, spacing, _ = node_tables()
    h = step_length
    depth, rows, cols = init_hbm.shape
    depth_c, rows_c = depth // 2, rows // 2
    half = rows_c // 2
    width = send_1.shape[1]
    length = send_1.shape[2]
    solvers = width // 8
    span = nt // groups
    own = pl.ds(HALO, depth)
    t, s = lax.axis_index("tm"), lax.axis_index("space")
    group = t // span
    base = group * span
    above, below = lax.rem(s + 1, ns), lax.rem(s + ns - 1, ns)
    per = max(1, solvers // ns)
    lead = base + (span - per) // 2
    mine = (t - lead) * ns + s
    is_solver = (t >= lead) & (mine < solvers)
    all_solve = solvers == span * ns

    def place_of(a):
        return lead + a // ns, lax.rem(a, ns)

    barrier = pltpu.get_barrier_semaphore()

    def signal_along(sem, step):
        @pl.when(t + step < nt)
        def _():
            pl.semaphore_signal(sem, inc=1, device_id=(t + step, s), device_id_type=MESH)

        @pl.when(t >= step)
        def _():
            pl.semaphore_signal(sem, inc=1, device_id=(t - step, s), device_id_type=MESH)

    def sides(step):
        return jnp.where(t + step < nt, 1, 0) + jnp.where(t >= step, 1, 0)

    signal_along(barrier, 1)
    for i in range(1, ns):
        pl.semaphore_signal(
            barrier, inc=1, device_id=(t, lax.rem(s + i, ns)), device_id_type=MESH
        )
    load = pltpu.make_async_copy(u_hbm.at[0], u.at[:, own], load_sem)
    load.start()
    tables = [
        pltpu.make_async_copy(source, target, table_sem.at[i])
        for i, (source, target) in enumerate(
            ((ytab_hbm.at[0], ytab), (ytab_hbm.at[1], ytab_back), (xtab_hbm, xtab), (ztab_hbm, ztab), (inv_hbm, inv))
        )
    ]
    for copy in tables:
        copy.start()
    local_start = pltpu.make_async_copy(init_hbm, w.at[0, own], start_sem)

    @pl.when(t == 0)
    def _():
        local_start.start()

    with jax.named_scope("barrier"):
        pl.semaphore_wait(barrier, ns - 1 + sides(1))

    lows, highs = pl.ds(0, HALO), pl.ds(HALO + depth, HALO)
    first, last = pl.ds(0, HALO), pl.ds(depth - HALO, HALO)

    def remote(source, target, send, recv, place):
        return pltpu.make_async_remote_copy(
            src_ref=source, dst_ref=target, send_sem=send, recv_sem=recv,
            device_id=place, device_id_type=MESH,
        )

    after = jnp.minimum(t + 1, nt - 1)
    node = u_hbm.at[0, 4]
    steps = depth // BLOCK - 2

    def start_piece(i, begin, size):
        return remote(
            node.at[pl.ds(begin, size)], w.at[0, pl.ds(HALO + begin, size)],
            start_send.at[i], start_recv.at[i], (after, s),
        )

    def inner(i):
        return start_piece(4 + i, HALO + i * BLOCK, BLOCK)

    start_edges = [start_piece(0, 0, HALO), start_piece(1, depth - HALO, HALO)]
    final = start_piece(4 + steps, HALO + steps * BLOCK, depth - 2 * HALO - steps * BLOCK)
    starts = start_edges + [inner(i) for i in range(steps)] + [final]

    def edges(source, shift):
        return [
            remote(
                source.at[pl.ds(shift + depth - HALO, HALO)], w.at[0, lows],
                start_send.at[2], start_recv.at[2], (t, above),
            ),
            remote(
                source.at[pl.ds(shift, HALO)], w.at[0, highs],
                start_send.at[3], start_recv.at[3], (t, below),
            ),
        ]

    inits, passed = edges(init_hbm, 0), edges(w.at[0], HALO)
    halos = [
        remote(u_hbm.at[0, :, last], u.at[:, lows], halo_send.at[0], halo_recv.at[0], (t, above)),
        remote(u_hbm.at[0, :, first], u.at[:, highs], halo_send.at[1], halo_recv.at[1], (t, below)),
    ]

    @pl.when(t < nt - 1)
    def _():
        for copy in starts:
            copy.start()

    for copy in halos:
        copy.start()

    @pl.when(t == 0)
    def _():
        for copy in inits:
            copy.start()

    signal_along(known_sem.at[0], 1)
    rounds = known_sem.shape[0]

    def hear(i):
        pl.semaphore_wait(known_sem.at[i], sides(2 ** i))
        if i + 1 < rounds:
            signal_along(known_sem.at[i + 1], 2 ** (i + 1))

    with jax.named_scope("w_edges"):
        @pl.when(t > 0)
        def _():
            start_edges[1].wait_recv()
            passed[0].start()
            start_edges[0].wait_recv()
            passed[1].start()

    if rounds > 1:
        hear(0)

    with jax.named_scope("w_halo"):
        load.wait()
        for copy in halos:
            copy.wait_recv()

    if rounds > 2:
        hear(1)

    def fold_block(i, carry):
        z = 1 + i * BLOCK
        parts = [force(u[k, pl.ds(z - 1, BLOCK + 2)]) for k in range(5)]
        for j in range(4):
            total = None
            for k in range(5):
                weight = h * integ[j][k] - (h * spacing[j] if j == k else 0.0)
                term = weight * parts[k]
                total = term if total is None else total + term
            corr[j, pl.ds(z, BLOCK)] = total
        return carry

    with jax.named_scope("fold"):
        lax.fori_loop(0, (depth + 2 * HALO - 2) // BLOCK, fold_block, 0)

    for i in range(2, rounds - 1):
        hear(i)

    @pl.when(t == 0)
    def _():
        local_start.wait()

    for copy in inits:
        copy.wait_recv()

    def advance(m, padded, here):
        now = force(padded)
        forces[m, here] = now
        result = padded[1:-1] + (h * spacing[m]) * now + corr[m, here]
        w[m + 1, here] = result
        return result

    plane = rows * depth_c

    def step(begin, count):
        reached = None
        for m in range(5):
            at = begin - m
            if m == 0:
                padded = w[0, pl.ds(at - 1, count + 2)]
            else:
                padded = jnp.concatenate([w[m, pl.ds(at - 1, 2)], reached], axis=0)
            if m < 4:
                reached = advance(m, padded, pl.ds(at, count))
        here = pl.ds(at, count)
        now, end = force(padded), padded[1:-1]
        middle = w[2, here]
        olds = [forces[m, here] for m in range(4)] + [now]
        outs = []
        for a in range(2):
            total = (w[0, here] - middle) if a == 0 else (middle - end)
            for m in range(5):
                total = total + (h * (integ[2 * a][m] + integ[2 * a + 1][m])) * olds[m]
            outs.append(total)
        outs.append(end - u[4, here])
        for f in range(3):
            pair = outs[f].reshape(count // 2, 2, rows, cols)
            pair = pair[:, 0] + pair[:, 1]
            to = f * plane + (at - HALO) // 2 * rows
            if not isinstance(to, int):
                to = pl.multiple_of(to, 8)
            restricted[pl.ds(to, count // 2 * rows), :] = pair.reshape(count // 2 * rows, cols)

    with jax.named_scope("prologue"):
        for m in range(4):
            count = BLOCK - 2 * m
            advance(m, w[m, pl.ds(m, count + 2)], pl.ds(1 + m, count))

    def main_step(i, carry):
        @pl.when(t > 0)
        def _():
            inner(i).wait_recv()

        step(HALO + 4 + i * BLOCK, BLOCK)
        return carry

    with jax.named_scope("steps"):
        lax.fori_loop(0, steps, main_step, 0)

    with jax.named_scope("w_final"):
        @pl.when(t > 0)
        def _():
            final.wait_recv()

    with jax.named_scope("tail"):
        step(HALO + 4 + steps * BLOCK, 2 * BLOCK)

    with jax.named_scope("fwd"):
        filled = 3 * depth_c
        for copy in tables:
            copy.wait()
        slabs = []
        for x in range(rows_c):
            even = restricted[pl.ds(2 * x, filled, stride=rows), :]
            odd = restricted[pl.ds(2 * x + 1, filled, stride=rows), :]
            slabs.append(even + odd)
        pairs = [
            jnp.concatenate([slabs[x] + slabs[x + half], slabs[x] - slabs[x + half]], axis=1)
            for x in range(half)
        ]
        turned = product(halves(jnp.concatenate(pairs, axis=0)), (ytab[0], ytab[1]), ((1,), (0,)))
        parts = [turned[x * filled:(x + 1) * filled] for x in range(half)]
        mixed = []
        for j in range(half):
            total = None
            for x in range(half):
                term = xtab[pl.ds(j * half + x, 1), :] * parts[x]
                total = term if total is None else total + term
            mixed.append(total)
        for f in range(3):
            field = jnp.concatenate([mixed[j][f * depth_c:(f + 1) * depth_c] for j in range(half)], axis=0)
            if length > half * depth_c:
                field = jnp.concatenate([field, jnp.zeros((length - half * depth_c, width), jnp.float32)], axis=0)
            send_1[f] = jnp.transpose(field)

    slot = s * span + (t - base)
    hear(rounds - 1)

    def spread(i, carry):
        a = lax.rem(s * per + i, solvers)
        to_t, to_s = place_of(a)

        @pl.when((to_t != t) | (to_s != s))
        def _():
            remote(
                send_1.at[:, pl.ds(pl.multiple_of(a * 8, 8), 8)], recv_1.at[slot],
                sems.at[0], sems.at[1], (to_t, to_s),
            ).start()

        return carry

    with jax.named_scope("issue1"):
        lax.fori_loop(0, solvers, spread, 0)

    def when_solver(body):
        if all_solve:
            body()
        else:
            pl.when(is_solver)(body)

    def bytes_wait(ref, count, sem):
        if count > 0:
            part = ref.at[pl.ds(0, count)]
            pltpu.make_async_copy(part, part, sem).wait()

    def carry_copy(to_t):
        return remote(carry_out, carry_in, sems.at[4], sems.at[5], (to_t, s))

    def solve():
        at = pl.multiple_of(mine * 8, 8)
        recv_1[slot] = send_1[:, pl.ds(at, 8)]
        factor = inv[pl.ds(at, 8), :]
        with jax.named_scope("w_recv1"):
            bytes_wait(recv_1, span * ns - 1, sems.at[1])
        with jax.named_scope("solve"):
            joined = jnp.concatenate(
                [
                    jnp.concatenate(
                        [recv_1[pl.ds(q * span, span), f].reshape(span * 8, length) for q in range(ns)], axis=1
                    )
                    for f in range(3)
                ],
                axis=0,
            )
            spectra = product(halves(joined), (ztab[0], ztab[1]), ((1,), (0,)))
            height = span * 8

            if groups > 1:
                carry_in_zero = group == 0

                @pl.when(carry_in_zero)
                def _():
                    carry_in[...] = jnp.zeros(carry_in.shape, jnp.float32)

                @pl.when(group > 0)
                def _():
                    carry_copy(t).wait_recv()

                begin = carry_in[...]
            else:
                begin = jnp.zeros(factor.shape, jnp.float32)
            fields = [[], [], []]
            for n in range(span):
                part = [spectra[f * height + n * 8:f * height + n * 8 + 8] for f in range(3)]
                middle = (begin + part[0]) * factor
                finish = (middle + part[1]) * factor
                for f, value in enumerate((begin, middle, finish)):
                    fields[f].append(value)
                begin = finish + part[2]
            if groups > 1:
                carry_out[...] = begin

                @pl.when(group < groups - 1)
                def _():
                    carry_copy(t + span).start()

            solved = jnp.concatenate([value for field in fields for value in field], axis=0)
            back = product(halves(solved), (ztab[0], ztab[1]), ((1,), (1,)))
            for f in range(3):
                for q in range(ns):
                    send_2[pl.ds(q * span, span), f] = back[
                        f * height:(f + 1) * height, q * length:(q + 1) * length
                    ].reshape(span, 8, length)

        def give(i, carry):
            other = lax.rem(slot + i, span * ns)
            remote(
                send_2.at[other], recv_2.at[mine], sems.at[2], sems.at[3],
                (base + lax.rem(other, span), other // span),
            ).start()
            return carry

        with jax.named_scope("issue2"):
            lax.fori_loop(1, span * ns, give, 0)
        recv_2[mine] = send_2[slot]
        with jax.named_scope("w_recv2"):
            bytes_wait(recv_2, solvers - 1, sems.at[3])

    when_solver(solve)
    if not all_solve:
        @pl.when(jnp.logical_not(is_solver))
        def _():
            with jax.named_scope("w_recv2"):
                bytes_wait(recv_2, solvers, sems.at[3])

    with jax.named_scope("inv"):
        returned = [jnp.transpose(recv_2[:, f].reshape(width, length)) for f in range(3)]
        mixed = [
            jnp.concatenate([returned[f][j * depth_c:(j + 1) * depth_c] for f in range(3)], axis=0)
            for j in range(half)
        ]
        parts = []
        for x in range(half):
            total = None
            for j in range(half):
                term = xtab[pl.ds(j * half + x, 1), :] * mixed[j]
                total = term if total is None else total + term
            parts.append(total)
        coarse = product(halves(jnp.concatenate(parts, axis=0)), (ytab_back[0], ytab_back[1]), ((1,), (1,)))
        for x in range(rows_c):
            part = coarse[(x % half) * filled:(x % half + 1) * filled, (x // half) * cols:(x // half + 1) * cols]
            for side in range(2):
                up[pl.ds(2 * x + side, filled, stride=rows), :] = part

    for copy in halos:
        copy.wait_send()

    @pl.when(t < nt - 1)
    def _():
        for copy in starts:
            copy.wait_send()

    for copy in inits:
        copy.wait_send()

    def sent():
        bytes_wait(recv_1, solvers - 1, sems.at[0])
        bytes_wait(send_2, span * ns - 1, sems.at[2])
        if groups > 1:
            @pl.when(group < groups - 1)
            def _():
                carry_copy(t).wait_send()

    when_solver(sent)
    if not all_solve:
        @pl.when(jnp.logical_not(is_solver))
        def _():
            bytes_wait(recv_2, solvers, sems.at[0])


def finish(w, up, out, staged, sems):
    _, _, interp = node_tables()
    depth, rows, cols = out.shape[2:]
    plane = rows * (depth // 2)
    part = depth // PARTS

    def give(p):
        return pltpu.make_async_copy(staged.at[p], out.at[0, :, pl.ds(p * part, part)], sems.at[p])

    for p in range(PARTS):
        def add_block(i, carry, p=p):
            begin = p * part + i * PIECE
            count = PIECE // 2 * rows
            fields = [
                up[pl.ds(pl.multiple_of(c * plane + begin // 2 * rows, 8), count), :] for c in range(3)
            ]
            for m in range(5):
                total = None
                for c in range(3):
                    if abs(interp[m][c]) < 1e-14:
                        continue
                    term = fields[c]
                    if abs(interp[m][c] - 1.0) > 1e-14:
                        term = interp[m][c] * term
                    total = term if total is None else total + term
                total = total.reshape(PIECE // 2, 1, rows, cols)
                total = jnp.broadcast_to(total, (PIECE // 2, 2, rows, cols)).reshape(PIECE, rows, cols)
                staged[p, m, pl.ds(i * PIECE, PIECE)] = w[m, pl.ds(HALO + begin, PIECE)] + total
            return carry

        lax.fori_loop(0, part // PIECE, add_block, 0)
        give(p).start()
    for p in range(PARTS):
        give(p).wait()


def shards(nt, ns, u_old, u_init):
    depth, rows, cols = u_init.shape
    depth_c, rows_c, cols_c = depth // 2, rows // 2, cols // 2
    half = rows_c // 2
    whole_c = depth_c * ns
    width = 2 * cols_c
    solvers = width // 8
    groups = GROUPS
    span = nt // groups
    length = -(-half * depth_c // 128) * 128
    extended = depth + 2 * HALO
    rounds = max(1, (nt - 1).bit_length())
    steps = depth // BLOCK - 2

    wide = np.repeat(hartley(cols_c), 2, axis=0)
    zero = np.zeros_like(wide)
    forth = 0.125 * np.block([[wide, zero], [zero, wide]])
    back = np.block([[wide, wide], [wide, -wide]])
    ytab = np.stack([two_parts(forth), two_parts(back)])
    wave_x = hartley(rows_c)
    xtab = np.zeros((half * half, width), np.float32)
    for j in range(half):
        for x in range(half):
            xtab[j * half + x, :cols_c] = wave_x[2 * j, x]
            xtab[j * half + x, cols_c:] = wave_x[2 * j + 1, x]
    wave_z = hartley(whole_c).reshape(ns, depth_c, whole_c)
    ztab = np.zeros((ns, length, half, whole_c))
    for j in range(half):
        ztab[:, j * depth_c:(j + 1) * depth_c, j] = wave_z
    ztab = two_parts(ztab.reshape(ns * length, half * whole_c))
    angle_z = 2.0 * np.cos(2.0 * np.pi * np.arange(whole_c) / whole_c)
    angle_x = 2.0 * np.cos(2.0 * np.pi * np.arange(rows_c) / rows_c)
    angle_y = 2.0 * np.cos(2.0 * np.pi * np.arange(cols_c) / cols_c)
    eigen = 0.25 * (
        angle_x.reshape(half, 2).T[:, None, :, None] + angle_y[None, :, None, None] + angle_z - 6.0
    )
    inv = (1.0 / (1.0 - 0.5 * step_length * diffusion * eigen)).astype(np.float32)
    inv = inv.reshape(width, half * whole_c)

    f32 = jnp.float32
    arrays = (u_old, u_init, ytab, xtab, ztab, inv)
    states, corrections = pl.pallas_call(
        functools.partial(kernel, nt, ns, groups),
        out_shape=(
            jax.ShapeDtypeStruct((5, extended, rows, cols), f32),
            jax.ShapeDtypeStruct((3 * depth_c * rows, cols), f32),
        ),
        in_specs=[pl.BlockSpec(memory_space=pltpu.HBM)] * 6,
        out_specs=(pl.BlockSpec(memory_space=pltpu.VMEM),) * 2,
        scratch_shapes=[
            pltpu.VMEM((5, extended, rows, cols), f32),
            pltpu.VMEM((4, extended, rows, cols), f32),
            pltpu.VMEM((4, extended, rows, cols), f32),
            pltpu.VMEM((3 * depth_c * rows, cols), f32),
            pltpu.VMEM(ytab.shape[1:], jnp.bfloat16),
            pltpu.VMEM(ytab.shape[1:], jnp.bfloat16),
            pltpu.VMEM(xtab.shape, f32),
            pltpu.VMEM(ztab.shape, jnp.bfloat16),
            pltpu.VMEM(inv.shape, f32),
            pltpu.VMEM((3, width, length), f32),
            pltpu.VMEM((span * ns, 3, 8, length), f32),
            pltpu.VMEM((span * ns, 3, 8, length), f32),
            pltpu.VMEM((solvers, 3, 8, length), f32),
            pltpu.VMEM((8, half * whole_c), f32),
            pltpu.VMEM((8, half * whole_c), f32),
            pltpu.SemaphoreType.DMA,
            pltpu.SemaphoreType.DMA((5,)),
            pltpu.SemaphoreType.DMA,
            pltpu.SemaphoreType.DMA((2,)),
            pltpu.SemaphoreType.DMA((2,)),
            pltpu.SemaphoreType.DMA((5 + steps,)),
            pltpu.SemaphoreType.DMA((5 + steps,)),
            pltpu.SemaphoreType.DMA((6,)),
            pltpu.SemaphoreType.REGULAR((rounds,)),
        ],
        compiler_params=pltpu.CompilerParams(
            collective_id=0, has_side_effects=True, vmem_limit_bytes=36000000
        ),
    )(*(pltpu.with_memory_space_constraint(a, pltpu.HBM) for a in arrays))
    return pl.pallas_call(
        finish,
        out_shape=jax.ShapeDtypeStruct((1, 5, depth, rows, cols), f32),
        in_specs=[pl.BlockSpec(memory_space=pltpu.VMEM)] * 2,
        out_specs=pl.BlockSpec(memory_space=pltpu.HBM),
        scratch_shapes=[
            pltpu.VMEM((PARTS, 5, depth // PARTS, rows, cols), f32),
            pltpu.SemaphoreType.DMA((PARTS,)),
        ],
        compiler_params=pltpu.CompilerParams(vmem_limit_bytes=16000000),
    )(states, corrections)


def solution(mesh):
    return jax.shard_map(
        functools.partial(shards, mesh.shape["tm"], mesh.shape["space"]),
        mesh=mesh,
        in_specs=(P("tm", None, "space", None, None), P("space", None, None)),
        out_specs=P("tm", None, "space", None, None),
        check_vma=False,
    )
```

time: 45.8 us -> 31.7 us (0.69)
  the two profiles are of different devices: /device:TPU:25 before, /device:TPU:17 now
where the time goes in v2:
time: 31.7 us; the launch traced here: 31.6 us
  Pallas kernels  31.6 us (100%)
    pallas_call x1, Pallas kernels, shards(): pl.pallas_call(functools.partial(kernel, nt, ns, groups), out_shape=(jax....  30 us
    pallas_call x1, Pallas kernels, shards(): pl.pallas_call(finish, out_shape=jax.ShapeDtypeStruct((1, 5, depth, rows,...  1.61 us

profile of v2, /device:TPU:17, one launch (start us, length us, event | category | flops | bytes accessed | tf_op | source)
XLA Modules:
  0.0 31.6 jit_solution(9569503739156007657)
XLA Ops:
  0.0 30.0 %shard_map.64 = (f32[5,74,16,128]{3,2,1,0:T(8,128)S(1)}, f32[1536,128]{1,0:T(8,128)S(1)}) custom-call(f32[1,5,64,16,128]{4,3,2,1,0:T(8,128)} %u_hbm.1, f32[64,16,128]{2,1,0:T(8,128)} %init_hbm.1, bf16[2,2,256,128]{3,2,1,0:T(8,128)(2,1)} %constant.8.clone.ytab_hbm, f32[16,128]{1,0:T(8,128)} %constant.9.clone.xtab_hbm, ...), custom_call_target="tpu_custom_call" | custom-call | tf_op jit(solution)/shard_map/pallas_call | solution.py:603
  30.0 1.6 %shard_map.65 = f32[1,5,64,16,128]{4,3,2,1,0:T(8,128)} custom-call(f32[5,74,16,128]{3,2,1,0:T(8,128)S(1)} %get-tuple-element.7.w, f32[1536,128]{1,0:T(8,128)S(1)} %get-tuple-element.8.up), custom_call_target="tpu_custom_call" | custom-call | tf_op jit(solution)/shard_map/pallas_call | solution.py:641

commit v3 on v2

--- a/solution.py
+++ b/solution.py
@@ -14,8 +14,6 @@
 reaction = 1.0
 HALO = 5
 BLOCK = 8
-PIECE = 4
-PARTS = 4
 GROUPS = 2
 MESH = pl.DeviceIdType.MESH
 
@@ -89,6 +87,11 @@
     return one(a[0], b[0]) + (one(a[0], b[1]) + one(a[1], b[0]))
 
 
+def far_first(flip):
+    hops = bin(flip[0]).count("1") + bin(flip[1] // 2).count("1")
+    return -(flip[1] // 2), -hops, -flip[0]
+
+
 def force(padded):
     field = padded[1:-1]
     rows, cols = field.shape[1:]
@@ -101,10 +104,10 @@
 
 def kernel(
     nt, ns, groups,
-    u_hbm, init_hbm, ytab_hbm, xtab_hbm, ztab_hbm, inv_hbm,
-    w, up,
-    u, corr, forces, restricted, ytab, ytab_back, xtab, ztab, inv,
-    send_1, recv_1, send_2, recv_2, carry_out, carry_in,
+    u_hbm, init_hbm, ytab_hbm, xtab_hbm, zback_hbm, zearly_hbm, zlate_hbm, inv_hbm,
+    w, recv_2, ytab_back, xtab,
+    u, corr, forces, restricted, ytab, zback, zearly, zlate, inv,
+    send_a, recv_a, staged, send_l, recv_l, send_2, carry_out, carry_in,
     load_sem, table_sem, start_sem, halo_send, halo_recv, start_send, start_recv,
     sems, known_sem,
 ):
@@ -113,8 +116,13 @@
     depth, rows, cols = init_hbm.shape
     depth_c, rows_c = depth // 2, rows // 2
     half = rows_c // 2
-    width = send_1.shape[1]
-    length = send_1.shape[2]
+    width = staged.shape[1]
+    length = send_2.shape[3]
+    late_c = BLOCK
+    blocks = length // (half * late_c)
+    middles = 1 if depth_c > 2 * late_c else 0
+    early_c = depth_c - (1 + middles) * late_c
+    tiles = send_a.shape[0]
     solvers = width // 8
     span = nt // groups
     own = pl.ds(HALO, depth)
@@ -155,7 +163,10 @@
     tables = [
         pltpu.make_async_copy(source, target, table_sem.at[i])
         for i, (source, target) in enumerate(
-            ((ytab_hbm.at[0], ytab), (ytab_hbm.at[1], ytab_back), (xtab_hbm, xtab), (ztab_hbm, ztab), (inv_hbm, inv))
+            (
+                (ytab_hbm.at[0], ytab), (ytab_hbm.at[1], ytab_back), (xtab_hbm, xtab), (zback_hbm, zback),
+                (zearly_hbm, zearly), (zlate_hbm, zlate), (inv_hbm, inv),
+            )
         )
     ]
     for copy in tables:
@@ -329,32 +340,22 @@
         step(HALO + 4 + i * BLOCK, BLOCK)
         return carry
 
-    with jax.named_scope("steps"):
-        lax.fori_loop(0, steps, main_step, 0)
-
-    with jax.named_scope("w_final"):
-        @pl.when(t > 0)
-        def _():
-            final.wait_recv()
-
-    with jax.named_scope("tail"):
-        step(HALO + 4 + steps * BLOCK, 2 * BLOCK)
-
-    with jax.named_scope("fwd"):
-        filled = 3 * depth_c
-        for copy in tables:
-            copy.wait()
+    def transformed(begin, count):
         slabs = []
         for x in range(rows_c):
-            even = restricted[pl.ds(2 * x, filled, stride=rows), :]
-            odd = restricted[pl.ds(2 * x + 1, filled, stride=rows), :]
-            slabs.append(even + odd)
+            fields = []
+            for f in range(3):
+                at = f * plane + begin * rows + 2 * x
+                even = restricted[pl.ds(at, count, stride=rows), :]
+                odd = restricted[pl.ds(at + 1, count, stride=rows), :]
+                fields.append(even + odd)
+            slabs.append(jnp.concatenate(fields, axis=0))
         pairs = [
             jnp.concatenate([slabs[x] + slabs[x + half], slabs[x] - slabs[x + half]], axis=1)
             for x in range(half)
         ]
         turned = product(halves(jnp.concatenate(pairs, axis=0)), (ytab[0], ytab[1]), ((1,), (0,)))
-        parts = [turned[x * filled:(x + 1) * filled] for x in range(half)]
+        parts = [turned[x * 3 * count:(x + 1) * 3 * count] for x in range(half)]
         mixed = []
         for j in range(half):
             total = None
@@ -362,30 +363,113 @@
                 term = xtab[pl.ds(j * half + x, 1), :] * parts[x]
                 total = term if total is None else total + term
             mixed.append(total)
-        for f in range(3):
-            field = jnp.concatenate([mixed[j][f * depth_c:(f + 1) * depth_c] for j in range(half)], axis=0)
-            if length > half * depth_c:
-                field = jnp.concatenate([field, jnp.zeros((length - half * depth_c, width), jnp.float32)], axis=0)
-            send_1[f] = jnp.transpose(field)
+        return [
+            jnp.concatenate([mixed[j][f * count:(f + 1) * count] for j in range(half)], axis=0)
+            for f in range(3)
+        ]
 
     slot = s * span + (t - base)
+
+    tau = t - base
+    paired = all_solve and span & (span - 1) == 0 and ns & (ns - 1) == 0
+
+    def flipped(value, mask):
+        for bit in range(mask.bit_length()):
+            if mask >> bit & 1:
+                value = value + (1 - 2 * (value // 2 ** bit % 2)) * 2 ** bit
+        return value
+
+    def flips():
+        return sorted(((a, b) for a in range(span) for b in range(ns) if a or b), key=far_first)
+
+    def spread(source_of, target, sem):
+        def go(a, to_t, to_s):
+            remote(
+                source_of(pl.ds(pl.multiple_of(a * 8, 8), 8)), target.at[slot],
+                sems.at[sem], sems.at[sem + 1], (to_t, to_s),
+            ).start()
+
+        if paired:
+            for flip_t, flip_s in flips():
+                to_tau, to_s = flipped(tau, flip_t), flipped(s, flip_s)
+                go(to_tau * ns + to_s, base + to_tau, to_s)
+        else:
+            def body(a, carry):
+                to_t, to_s = place_of(a)
+
+                @pl.when((to_t != t) | (to_s != s))
+                def _():
+                    go(a, to_t, to_s)
+
+                return carry
+
+            lax.fori_loop(0, solvers, body, 0)
+
+    def late(k):
+        high = half * late_c
+        for f, field in enumerate(transformed(early_c + k * late_c, late_c)):
+            staged[k, pl.ds(pl.multiple_of(lax.rem(f + s, blocks) * high, 8), high), :] = field
+        for f in range(3, blocks):
+            staged[k, pl.ds(pl.multiple_of(lax.rem(f + s, blocks) * high, 8), high), :] = jnp.zeros(
+                (high, width), jnp.float32
+            )
+        send_l[k] = jnp.transpose(staged[k])
+
+    early_steps = early_c * 2 // BLOCK
+    with jax.named_scope("steps"):
+        lax.fori_loop(0, early_steps, main_step, 0)
+
+    with jax.named_scope("fwd_a"):
+        for copy in tables:
+            copy.wait()
+        if early_c > 0:
+            together = transformed(0, early_c)
+            filled = half * early_c
+            per_tile = length // filled
+            for i in range(tiles):
+                parts = together[i * per_tile:(i + 1) * per_tile]
+                if len(parts) * filled < length:
+                    parts.append(jnp.zeros((length - len(parts) * filled, width), jnp.float32))
+                send_a[i] = jnp.transpose(jnp.concatenate(parts, axis=0))
+
     hear(rounds - 1)
-
-    def spread(i, carry):
-        a = lax.rem(s * per + i, solvers)
-        to_t, to_s = place_of(a)
-
-        @pl.when((to_t != t) | (to_s != s))
+    if early_c > 0:
+        with jax.named_scope("issue_a"):
+            spread(lambda r: send_a.at[:, r], recv_a, 0)
+
+    with jax.named_scope("steps_m"):
+        lax.fori_loop(early_steps, steps, main_step, 0)
+
+    if middles:
+        with jax.named_scope("fwd_m"):
+            late(0)
+        with jax.named_scope("issue_m"):
+            spread(lambda r: send_l.at[0, r], recv_l.at[0], 8)
+
+    with jax.named_scope("w_final"):
+        @pl.when(t > 0)
         def _():
-            remote(
-                send_1.at[:, pl.ds(pl.multiple_of(a * 8, 8), 8)], recv_1.at[slot],
-                sems.at[0], sems.at[1], (to_t, to_s),
-            ).start()
-
-        return carry
-
-    with jax.named_scope("issue1"):
-        lax.fori_loop(0, solvers, spread, 0)
+            final.wait_recv()
+
+    with jax.named_scope("tail"):
+        step(HALO + 4 + steps * BLOCK, 2 * BLOCK)
+
+    with jax.named_scope("fwd_b"):
+        late(middles)
+    with jax.named_scope("issue_b"):
+        spread(lambda r: send_l.at[middles, r], recv_l.at[middles], 6)
+
+    with jax.named_scope("sent"):
+        for copy in halos:
+            copy.wait_send()
+
+        @pl.when(t < nt - 1)
+        def _():
+            for copy in starts:
+                copy.wait_send()
+
+        for copy in inits:
+            copy.wait_send()
 
     def when_solver(body):
         if all_solve:
@@ -398,26 +482,76 @@
             part = ref.at[pl.ds(0, count)]
             pltpu.make_async_copy(part, part, sem).wait()
 
+    def forward_sent(count):
+        if early_c > 0:
+            bytes_wait(recv_a, count, sems.at[0])
+        if middles:
+            bytes_wait(recv_l.at[0], count, sems.at[8])
+        bytes_wait(recv_l.at[middles], count, sems.at[6])
+
     def carry_copy(to_t):
         return remote(carry_out, carry_in, sems.at[4], sems.at[5], (to_t, s))
 
     def solve():
         at = pl.multiple_of(mine * 8, 8)
-        recv_1[slot] = send_1[:, pl.ds(at, 8)]
+        if early_c > 0:
+            recv_a[slot] = send_a[:, pl.ds(at, 8)]
+        for k in range(middles + 1):
+            recv_l[k, slot] = send_l[k, pl.ds(at, 8), :]
         factor = inv[pl.ds(at, 8), :]
-        with jax.named_scope("w_recv1"):
-            bytes_wait(recv_1, span * ns - 1, sems.at[1])
+        spectra = None
+        tall = span * 8
+        if early_c > 0:
+            with jax.named_scope("w_recv_a"):
+                bytes_wait(recv_a, span * ns - 1, sems.at[1])
+            with jax.named_scope("z_a"):
+                filled = half * early_c
+                per_tile = length // filled
+                lane = lax.broadcasted_iota(jnp.int32, (tall, length), 1) // filled
+                fields = []
+                for f in range(3):
+                    columns = []
+                    for k in range(-(-ns // per_tile)):
+                        chosen = jnp.zeros((tall, length), jnp.float32)
+                        for g in range(min(per_tile, ns - k * per_tile)):
+                            q = k * per_tile + g
+                            value = recv_a[pl.ds(q * span, span), f // per_tile].reshape(tall, length)
+                            shift = (g - f % per_tile) * filled % length
+                            if shift:
+                                value = pltpu.roll(value, shift, 1)
+                            chosen = jnp.where(lane == g, value, chosen)
+                        columns.append(chosen)
+                    fields.append(jnp.concatenate(columns, axis=1))
+                spectra = product(halves(jnp.concatenate(fields, axis=0)), (zearly[0], zearly[1]), ((1,), (0,)))
+
+        def late_part(k):
+            high = half * late_c
+            arrived = [recv_l[k, pl.ds(q * span, span)].reshape(tall, length) for q in range(ns)]
+            lane = lax.broadcasted_iota(jnp.int32, (tall, length), 1) // high
+            fields = []
+            for f in range(3):
+                columns = []
+                for c in range(-(-ns // blocks)):
+                    chosen = jnp.zeros((tall, length), jnp.float32)
+                    for q in range(c * blocks, min(ns, (c + 1) * blocks)):
+                        chosen = jnp.where(lane == (f + q) % blocks, arrived[q], chosen)
+                    if f > 0:
+                        chosen = pltpu.roll(chosen, length - high * f, 1)
+                    columns.append(chosen)
+                fields.append(jnp.concatenate(columns, axis=1))
+            return product(halves(jnp.concatenate(fields, axis=0)), (zlate[k, 0], zlate[k, 1]), ((1,), (0,)))
+
+        if middles:
+            with jax.named_scope("w_recv_m"):
+                bytes_wait(recv_l.at[0], span * ns - 1, sems.at[9])
+            with jax.named_scope("z_m"):
+                more = late_part(0)
+                spectra = more if spectra is None else spectra + more
+        with jax.named_scope("w_recv_b"):
+            bytes_wait(recv_l.at[middles], span * ns - 1, sems.at[7])
         with jax.named_scope("solve"):
-            joined = jnp.concatenate(
-                [
-                    jnp.concatenate(
-                        [recv_1[pl.ds(q * span, span), f].reshape(span * 8, length) for q in range(ns)], axis=1
-                    )
-                    for f in range(3)
-                ],
-                axis=0,
-            )
-            spectra = product(halves(joined), (ztab[0], ztab[1]), ((1,), (0,)))
+            more = late_part(middles)
+            spectra = more if spectra is None else spectra + more
             height = span * 8
 
             if groups > 1:
@@ -449,25 +583,53 @@
                 def _():
                     carry_copy(t + span).start()
 
-            solved = jnp.concatenate([value for field in fields for value in field], axis=0)
-            back = product(halves(solved), (ztab[0], ztab[1]), ((1,), (1,)))
-            for f in range(3):
-                for q in range(ns):
-                    send_2[pl.ds(q * span, span), f] = back[
-                        f * height:(f + 1) * height, q * length:(q + 1) * length
-                    ].reshape(span, 8, length)
-
-        def give(i, carry):
-            other = lax.rem(slot + i, span * ns)
+            whole_c = zback.shape[1] // 2
+            rows_all = jnp.concatenate(
+                [
+                    jnp.concatenate([value[:, j * whole_c:(j + 1) * whole_c] for field in fields for value in field], axis=0)
+                    for j in range(half)
+                ],
+                axis=0,
+            )
+            upper, lower = halves(rows_all)
+            wide = lax.dot_general(
+                jnp.concatenate([upper, lower], axis=1), zback[...], (((1,), (0,)), ((), ())),
+                preferred_element_type=jnp.float32,
+            )
+            back = wide[:, :whole_c] + wide[:, whole_c:]
+            turned = []
+            for j in range(half):
+                part = back[j * 3 * height:(j + 1) * 3 * height]
+                turned.append(pltpu.roll(part, j * depth_c, 1) if j else part)
+            lane = lax.broadcasted_iota(jnp.int32, (3 * height, length), 1) // depth_c
+            for q in range(ns):
+                message = turned[half - 1]
+                for j in range(half - 1):
+                    message = jnp.where(lane == (q + j) % ns, turned[j], message)
+                for f in range(3):
+                    send_2[pl.ds(q * span, span), f] = message[f * height:(f + 1) * height].reshape(span, 8, length)
+
+        peers = span * ns
+
+        def go(to_tau, to_s):
             remote(
-                send_2.at[other], recv_2.at[mine], sems.at[2], sems.at[3],
-                (base + lax.rem(other, span), other // span),
+                send_2.at[to_s * span + to_tau], recv_2.at[mine], sems.at[2], sems.at[3],
+                (base + to_tau, to_s),
             ).start()
-            return carry
 
         with jax.named_scope("issue2"):
-            lax.fori_loop(1, span * ns, give, 0)
+            if paired:
+                for flip_t, flip_s in flips():
+                    go(flipped(tau, flip_t), flipped(s, flip_s))
+            else:
+                def give(i, carry):
+                    other = lax.rem(slot + i, peers)
+                    go(lax.rem(other, span), other // span)
+                    return carry
+
+                lax.fori_loop(1, peers, give, 0)
         recv_2[mine] = send_2[slot]
+        forward_sent(solvers - 1)
         with jax.named_scope("w_recv2"):
             bytes_wait(recv_2, solvers - 1, sems.at[3])
 
@@ -475,13 +637,41 @@
     if not all_solve:
         @pl.when(jnp.logical_not(is_solver))
         def _():
+            forward_sent(solvers)
             with jax.named_scope("w_recv2"):
                 bytes_wait(recv_2, solvers, sems.at[3])
 
-    with jax.named_scope("inv"):
-        returned = [jnp.transpose(recv_2[:, f].reshape(width, length)) for f in range(3)]
+    def sent():
+        bytes_wait(send_2, span * ns - 1, sems.at[2])
+        if groups > 1:
+            @pl.when(group < groups - 1)
+            def _():
+                carry_copy(t).wait_send()
+
+    when_solver(sent)
+
+
+def finish(w, recv, ytab, xtab, out, returned, up, result, sems):
+    _, _, interp = node_tables()
+    depth, rows, cols = out.shape[2:]
+    depth_c, rows_c = depth // 2, rows // 2
+    half = rows_c // 2
+    solvers, _, _, length = recv.shape
+    count = depth_c // up.shape[0]
+    s = lax.axis_index("space")
+    slabs = length // depth_c
+    for f in range(3):
+        returned[f] = jnp.transpose(recv[:, f].reshape(solvers * 8, length))
+    places = [lax.rem(s + j, slabs) * depth_c for j in range(half)]
+
+    def give(p):
+        return pltpu.make_async_copy(result.at[p], out.at[0, :, pl.ds(p * 2 * count, 2 * count)], sems.at[p])
+
+    for p in range(up.shape[0]):
         mixed = [
-            jnp.concatenate([returned[f][j * depth_c:(j + 1) * depth_c] for f in range(3)], axis=0)
+            jnp.concatenate(
+                [returned[f, pl.ds(pl.multiple_of(places[j] + p * count, 8), count), :] for f in range(3)], axis=0
+            )
             for j in range(half)
         ]
         parts = []
@@ -491,54 +681,14 @@
                 term = xtab[pl.ds(j * half + x, 1), :] * mixed[j]
                 total = term if total is None else total + term
             parts.append(total)
-        coarse = product(halves(jnp.concatenate(parts, axis=0)), (ytab_back[0], ytab_back[1]), ((1,), (1,)))
+        coarse = product(halves(jnp.concatenate(parts, axis=0)), (ytab[0], ytab[1]), ((1,), (1,)))
+        high = 3 * count
         for x in range(rows_c):
-            part = coarse[(x % half) * filled:(x % half + 1) * filled, (x // half) * cols:(x // half + 1) * cols]
+            part = coarse[(x % half) * high:(x % half + 1) * high, (x // half) * cols:(x // half + 1) * cols]
             for side in range(2):
-                up[pl.ds(2 * x + side, filled, stride=rows), :] = part
-
-    for copy in halos:
-        copy.wait_send()
-
-    @pl.when(t < nt - 1)
-    def _():
-        for copy in starts:
-            copy.wait_send()
-
-    for copy in inits:
-        copy.wait_send()
-
-    def sent():
-        bytes_wait(recv_1, solvers - 1, sems.at[0])
-        bytes_wait(send_2, span * ns - 1, sems.at[2])
-        if groups > 1:
-            @pl.when(group < groups - 1)
-            def _():
-                carry_copy(t).wait_send()
-
-    when_solver(sent)
-    if not all_solve:
-        @pl.when(jnp.logical_not(is_solver))
-        def _():
-            bytes_wait(recv_2, solvers, sems.at[0])
-
-
-def finish(w, up, out, staged, sems):
-    _, _, interp = node_tables()
-    depth, rows, cols = out.shape[2:]
-    plane = rows * (depth // 2)
-    part = depth // PARTS
-
-    def give(p):
-        return pltpu.make_async_copy(staged.at[p], out.at[0, :, pl.ds(p * part, part)], sems.at[p])
-
-    for p in range(PARTS):
-        def add_block(i, carry, p=p):
-            begin = p * part + i * PIECE
-            count = PIECE // 2 * rows
-            fields = [
-                up[pl.ds(pl.multiple_of(c * plane + begin // 2 * rows, 8), count), :] for c in range(3)
-            ]
+                up[p, pl.ds(2 * x + side, high, stride=rows), :] = part
+        for z in range(count):
+            fields = [up[p, pl.ds((f * count + z) * rows, rows), :] for f in range(3)]
             for m in range(5):
                 total = None
                 for c in range(3):
@@ -548,14 +698,10 @@
                     if abs(interp[m][c] - 1.0) > 1e-14:
                         term = interp[m][c] * term
                     total = term if total is None else total + term
-                total = total.reshape(PIECE // 2, 1, rows, cols)
-                total = jnp.broadcast_to(total, (PIECE // 2, 2, rows, cols)).reshape(PIECE, rows, cols)
-                staged[p, m, pl.ds(i * PIECE, PIECE)] = w[m, pl.ds(HALO + begin, PIECE)] + total
-            return carry
-
-        lax.fori_loop(0, part // PIECE, add_block, 0)
+                for side in range(2):
+                    result[p, m, 2 * z + side] = w[m, HALO + 2 * (p * count + z) + side] + total
         give(p).start()
-    for p in range(PARTS):
+    for p in range(up.shape[0]):
         give(p).wait()
 
 
@@ -585,10 +731,29 @@
             xtab[j * half + x, :cols_c] = wave_x[2 * j, x]
             xtab[j * half + x, cols_c:] = wave_x[2 * j + 1, x]
     wave_z = hartley(whole_c).reshape(ns, depth_c, whole_c)
-    ztab = np.zeros((ns, length, half, whole_c))
+    late_c = BLOCK
+    blocks = length // (half * late_c)
+    sets = -(-ns // blocks)
+    middles = 1 if depth_c > 2 * late_c else 0
+    early_c = depth_c - (1 + middles) * late_c
+    per_tile = length // (half * early_c) if early_c else 1
+    tiles = -(-3 // per_tile) if early_c else 1
+    early_sets = -(-ns // per_tile)
+    zearly = np.zeros((early_sets, length, half * whole_c))
+    zlate = np.zeros((middles + 1, sets * blocks, half, late_c, half, whole_c))
     for j in range(half):
-        ztab[:, j * depth_c:(j + 1) * depth_c, j] = wave_z
-    ztab = two_parts(ztab.reshape(ns * length, half * whole_c))
+        for q in range(ns if early_c else 0):
+            row = q % per_tile * half * early_c + j * early_c
+            zearly[q // per_tile, row:row + early_c, j * whole_c:(j + 1) * whole_c] = wave_z[q, :early_c]
+        for k in range(middles + 1):
+            begin = early_c + k * late_c
+            zlate[k, :ns, j, :, j] = wave_z[:, begin:begin + late_c]
+    zearly = two_parts(zearly.reshape(early_sets * length, half * whole_c))
+    if early_c == 0:
+        zearly = zearly[:, :16]
+    zlate = np.stack([two_parts(part.reshape(sets * length, half * whole_c)) for part in zlate])
+    wave = two_parts(hartley(whole_c))
+    zback = np.block([[wave[0], wave[1]], [wave[0], np.zeros_like(wave[0])]])
     angle_z = 2.0 * np.cos(2.0 * np.pi * np.arange(whole_c) / whole_c)
     angle_x = 2.0 * np.cos(2.0 * np.pi * np.arange(rows_c) / rows_c)
     angle_y = 2.0 * np.cos(2.0 * np.pi * np.arange(cols_c) / cols_c)
@@ -599,39 +764,44 @@
     inv = inv.reshape(width, half * whole_c)
 
     f32 = jnp.float32
-    arrays = (u_old, u_init, ytab, xtab, ztab, inv)
-    states, corrections = pl.pallas_call(
+    bf16 = jnp.bfloat16
+    arrays = (u_old, u_init, ytab, xtab, zback, zearly, zlate, inv)
+    handed = pl.pallas_call(
         functools.partial(kernel, nt, ns, groups),
         out_shape=(
             jax.ShapeDtypeStruct((5, extended, rows, cols), f32),
-            jax.ShapeDtypeStruct((3 * depth_c * rows, cols), f32),
+            jax.ShapeDtypeStruct((solvers, 3, 8, length), f32),
+            jax.ShapeDtypeStruct(ytab.shape[1:], bf16),
+            jax.ShapeDtypeStruct(xtab.shape, f32),
         ),
-        in_specs=[pl.BlockSpec(memory_space=pltpu.HBM)] * 6,
-        out_specs=(pl.BlockSpec(memory_space=pltpu.VMEM),) * 2,
+        in_specs=[pl.BlockSpec(memory_space=pltpu.HBM)] * len(arrays),
+        out_specs=(pl.BlockSpec(memory_space=pltpu.VMEM),) * 4,
         scratch_shapes=[
             pltpu.VMEM((5, extended, rows, cols), f32),
             pltpu.VMEM((4, extended, rows, cols), f32),
             pltpu.VMEM((4, extended, rows, cols), f32),
             pltpu.VMEM((3 * depth_c * rows, cols), f32),
-            pltpu.VMEM(ytab.shape[1:], jnp.bfloat16),
-            pltpu.VMEM(ytab.shape[1:], jnp.bfloat16),
-            pltpu.VMEM(xtab.shape, f32),
-            pltpu.VMEM(ztab.shape, jnp.bfloat16),
+            pltpu.VMEM(ytab.shape[1:], bf16),
+            pltpu.VMEM(zback.shape, bf16),
+            pltpu.VMEM(zearly.shape, bf16),
+            pltpu.VMEM(zlate.shape, bf16),
             pltpu.VMEM(inv.shape, f32),
-            pltpu.VMEM((3, width, length), f32),
+            pltpu.VMEM((tiles, width, length), f32),
+            pltpu.VMEM((span * ns, tiles, 8, length), f32),
+            pltpu.VMEM((middles + 1, length, width), f32),
+            pltpu.VMEM((middles + 1, width, length), f32),
+            pltpu.VMEM((middles + 1, span * ns, 8, length), f32),
             pltpu.VMEM((span * ns, 3, 8, length), f32),
-            pltpu.VMEM((span * ns, 3, 8, length), f32),
-            pltpu.VMEM((solvers, 3, 8, length), f32),
             pltpu.VMEM((8, half * whole_c), f32),
             pltpu.VMEM((8, half * whole_c), f32),
             pltpu.SemaphoreType.DMA,
-            pltpu.SemaphoreType.DMA((5,)),
+            pltpu.SemaphoreType.DMA((7,)),
             pltpu.SemaphoreType.DMA,
             pltpu.SemaphoreType.DMA((2,)),
             pltpu.SemaphoreType.DMA((2,)),
             pltpu.SemaphoreType.DMA((5 + steps,)),
             pltpu.SemaphoreType.DMA((5 + steps,)),
-            pltpu.SemaphoreType.DMA((6,)),
+            pltpu.SemaphoreType.DMA((10,)),
             pltpu.SemaphoreType.REGULAR((rounds,)),
         ],
         compiler_params=pltpu.CompilerParams(
@@ -641,14 +811,16 @@
     return pl.pallas_call(
         finish,
         out_shape=jax.ShapeDtypeStruct((1, 5, depth, rows, cols), f32),
-        in_specs=[pl.BlockSpec(memory_space=pltpu.VMEM)] * 2,
+        in_specs=[pl.BlockSpec(memory_space=pltpu.VMEM)] * 4,
         out_specs=pl.BlockSpec(memory_space=pltpu.HBM),
         scratch_shapes=[
-            pltpu.VMEM((PARTS, 5, depth // PARTS, rows, cols), f32),
-            pltpu.SemaphoreType.DMA((PARTS,)),
+            pltpu.VMEM((3, length, width), f32),
+            pltpu.VMEM((depth_c // 8, 3 * 8 * rows, cols), f32),
+            pltpu.VMEM((depth_c // 8, 5, 16, rows, cols), f32),
+            pltpu.SemaphoreType.DMA((depth_c // 8,)),
         ],
         compiler_params=pltpu.CompilerParams(vmem_limit_bytes=16000000),
-    )(states, corrections)
+    )(*handed)
 
 
 def solution(mesh):

time: 31.7 us -> 29.6 us (0.934)
  Pallas kernels: 31.6 us -> 29.5 us
    pallas_call x1, Pallas kernels: 30 us -> 27.4 us  [shards(): pl.pallas_call(functools.partial(kernel, nt, ns, groups), out_shape=(jax....]
    pallas_call x1, Pallas kernels: 1.61 us -> 2.08 us  [shards(): pl.pallas_call(finish, out_shape=jax.ShapeDtypeStruct((1, 5, depth, rows,...]
where the time goes in v3:
time: 29.6 us; the launch traced here: 29.5 us
  Pallas kernels  29.5 us (100%)
    pallas_call x1, Pallas kernels, shards(): pl.pallas_call(functools.partial(kernel, nt, ns, groups), out_shape=(jax....  27.4 us
    pallas_call x1, Pallas kernels, shards(): pl.pallas_call(finish, out_shape=jax.ShapeDtypeStruct((1, 5, depth, rows,...  2.08 us

profile of v3, /device:TPU:17, one launch (start us, length us, event | category | flops | bytes accessed | tf_op | source)
XLA Modules:
  0.0 29.5 jit_solution(10103899834357271413)
XLA Ops:
  0.0 27.4 %shard_map.82 = (f32[5,74,16,128]{3,2,1,0:T(8,128)S(1)}, f32[16,3,8,128]{3,2,1,0:T(8,128)S(1)}, bf16[2,256,128]{2,1,0:T(8,128)(2,1)S(1)}, f32[16,128]{1,0:T(8,128)S(1)}) custom-call(f32[1,5,64,16,128]{4,3,2,1,0:T(8,128)} %u_hbm.1, f32[64,16,128]{2,1,0:T(8,128)} %init_hbm.1, bf16[2,2,256,128]{3,2,1,0:T(8,128)(2,1)} %constant.12.clone.ytab_hbm, ...), custom_call_target="tpu_custom_call" | custom-call | tf_op jit(solution)/shard_map/pallas_call | solution.py:769
  27.4 2.1 %shard_map.83 = f32[1,5,64,16,128]{4,3,2,1,0:T(8,128)} custom-call(f32[5,74,16,128]{3,2,1,0:T(8,128)S(1)} %get-tuple-element.9.w, f32[16,3,8,128]{3,2,1,0:T(8,128)S(1)} %get-tuple-element.10.recv, bf16[2,256,128]{2,1,0:T(8,128)(2,1)S(1)} %get-tuple-element.11.ytab, f32[16,128]{1,0:T(8,128)S(1)} %get-tuple-element.12.xtab), custom_call_target="tpu_custom_call" | custom-call | tf_op jit(solution)/shard_map/pallas_call | solution.py:811

commit v4 on v3

--- a/solution.py
+++ b/solution.py
@@ -87,6 +87,28 @@
     return one(a[0], b[0]) + (one(a[0], b[1]) + one(a[1], b[0]))
 
 
+def tables_of(half_tab, width, whole_c, middles, late):
+    rows = 2 * width
+    early = half_tab.shape[0] - 2 * rows - (middles + 1) * 2 * late
+
+    def forth(i):
+        return half_tab[pl.ds(i * rows, rows), pl.ds(0, width)]
+
+    def back(i):
+        return half_tab[pl.ds(i * rows, rows), pl.ds(width, width)]
+
+    def z_back():
+        return half_tab[pl.ds(0, 2 * whole_c), pl.ds(2 * width, 2 * whole_c)]
+
+    def z_early(i):
+        return half_tab[pl.ds(2 * rows + i * (early // 2), early // 2), :]
+
+    def z_late(k, i):
+        return half_tab[pl.ds(2 * rows + early + (2 * k + i) * late, late), :]
+
+    return forth, back, z_back, z_early, z_late
+
+
 def far_first(flip):
     hops = bin(flip[0]).count("1") + bin(flip[1] // 2).count("1")
     return -(flip[1] // 2), -hops, -flip[0]
@@ -104,11 +126,11 @@
 
 def kernel(
     nt, ns, groups,
-    u_hbm, init_hbm, ytab_hbm, xtab_hbm, zback_hbm, zearly_hbm, zlate_hbm, inv_hbm,
-    w, recv_2, ytab_back, xtab,
-    u, corr, forces, restricted, ytab, zback, zearly, zlate, inv,
+    u_hbm, init_hbm, half_tab_hbm, full_tab_hbm,
+    w, recv_2, half_tab, full_tab,
+    u, corr, forces, restricted,
     send_a, recv_a, staged, send_l, recv_l, send_2, carry_out, carry_in,
-    load_sem, table_sem, start_sem, halo_send, halo_recv, start_send, start_recv,
+    load_sem, table_sem, start_sem, early_send, edge_recv, start_recv,
     sems, known_sem,
 ):
     integ, spacing, _ = node_tables()
@@ -123,6 +145,10 @@
     middles = 1 if depth_c > 2 * late_c else 0
     early_c = depth_c - (1 + middles) * late_c
     tiles = send_a.shape[0]
+    whole_c = depth_c * ns
+    extended = depth + 2 * HALO
+    ytab, _, zback, zearly, zlate = tables_of(half_tab, width, whole_c, middles, -(-ns // blocks) * length)
+    inv, xtab = full_tab.at[pl.ds(0, width)], full_tab.at[pl.ds(width, half * half), pl.ds(0, width)]
     solvers = width // 8
     span = nt // groups
     own = pl.ds(HALO, depth)
@@ -161,13 +187,8 @@
     load = pltpu.make_async_copy(u_hbm.at[0], u.at[:, own], load_sem)
     load.start()
     tables = [
-        pltpu.make_async_copy(source, target, table_sem.at[i])
-        for i, (source, target) in enumerate(
-            (
-                (ytab_hbm.at[0], ytab), (ytab_hbm.at[1], ytab_back), (xtab_hbm, xtab), (zback_hbm, zback),
-                (zearly_hbm, zearly), (zlate_hbm, zlate), (inv_hbm, inv),
-            )
-        )
+        pltpu.make_async_copy(half_tab_hbm, half_tab, table_sem.at[0]),
+        pltpu.make_async_copy(full_tab_hbm, full_tab, table_sem.at[1]),
     ]
     for copy in tables:
         copy.start()
@@ -192,36 +213,44 @@
     after = jnp.minimum(t + 1, nt - 1)
     node = u_hbm.at[0, 4]
     steps = depth // BLOCK - 2
-
-    def start_piece(i, begin, size):
+    doubles = early_c // BLOCK
+    singles = steps - 2 * doubles
+
+    def start_piece(sem, begin, size):
         return remote(
             node.at[pl.ds(begin, size)], w.at[0, pl.ds(HALO + begin, size)],
-            start_send.at[i], start_recv.at[i], (after, s),
+            early_send, sem, (after, s),
         )
 
-    def inner(i):
-        return start_piece(4 + i, HALO + i * BLOCK, BLOCK)
-
-    start_edges = [start_piece(0, 0, HALO), start_piece(1, depth - HALO, HALO)]
-    final = start_piece(4 + steps, HALO + steps * BLOCK, depth - 2 * HALO - steps * BLOCK)
-    starts = start_edges + [inner(i) for i in range(steps)] + [final]
+    def inner(i, size, base_chunk):
+        return start_piece(start_recv.at[base_chunk + i], HALO + (2 * doubles if base_chunk else 0) * BLOCK + i * size, size)
+
+    def planes_wait(count, sem):
+        whole = next(k for k in range(1, 6) if count % k == 0 and count // k <= extended)
+        part = u.at[pl.ds(0, whole), pl.ds(0, count // whole)]
+        pltpu.make_async_copy(part, part, sem).wait()
+
+    start_edges = [start_piece(edge_recv.at[0], 0, HALO), start_piece(edge_recv.at[0], depth - HALO, HALO)]
+    final = start_piece(start_recv.at[doubles + singles], HALO + steps * BLOCK, depth - 2 * HALO - steps * BLOCK)
+    starts = start_edges + [inner(i, 2 * BLOCK, 0) for i in range(doubles)]
+    starts += [inner(i, BLOCK, doubles) for i in range(singles)] + [final]
 
     def edges(source, shift):
         return [
             remote(
                 source.at[pl.ds(shift + depth - HALO, HALO)], w.at[0, lows],
-                start_send.at[2], start_recv.at[2], (t, above),
+                early_send, edge_recv.at[1], (t, above),
             ),
             remote(
                 source.at[pl.ds(shift, HALO)], w.at[0, highs],
-                start_send.at[3], start_recv.at[3], (t, below),
+                early_send, edge_recv.at[1], (t, below),
             ),
         ]
 
     inits, passed = edges(init_hbm, 0), edges(w.at[0], HALO)
     halos = [
-        remote(u_hbm.at[0, :, last], u.at[:, lows], halo_send.at[0], halo_recv.at[0], (t, above)),
-        remote(u_hbm.at[0, :, first], u.at[:, highs], halo_send.at[1], halo_recv.at[1], (t, below)),
+        remote(u_hbm.at[0, :, last], u.at[:, lows], early_send, load_sem, (t, above)),
+        remote(u_hbm.at[0, :, first], u.at[:, highs], early_send, load_sem, (t, below)),
     ]
 
     @pl.when(t < nt - 1)
@@ -248,18 +277,15 @@
     with jax.named_scope("w_edges"):
         @pl.when(t > 0)
         def _():
-            start_edges[1].wait_recv()
-            passed[0].start()
-            start_edges[0].wait_recv()
-            passed[1].start()
+            planes_wait(2 * HALO, edge_recv.at[0])
+            for copy in passed:
+                copy.start()
 
     if rounds > 1:
         hear(0)
 
     with jax.named_scope("w_halo"):
-        load.wait()
-        for copy in halos:
-            copy.wait_recv()
+        pltpu.make_async_copy(u, u, load_sem).wait()
 
     if rounds > 2:
         hear(1)
@@ -286,8 +312,7 @@
     def _():
         local_start.wait()
 
-    for copy in inits:
-        copy.wait_recv()
+    planes_wait(2 * HALO, edge_recv.at[1])
 
     def advance(m, padded, here):
         now = force(padded)
@@ -332,13 +357,18 @@
             count = BLOCK - 2 * m
             advance(m, w[m, pl.ds(m, count + 2)], pl.ds(1 + m, count))
 
-    def main_step(i, carry):
-        @pl.when(t > 0)
-        def _():
-            inner(i).wait_recv()
-
-        step(HALO + 4 + i * BLOCK, BLOCK)
-        return carry
+    def main_steps(count, size, base_chunk):
+        first_z = HALO + 4 + (2 * doubles if base_chunk else 0) * BLOCK
+
+        def body(i, carry):
+            @pl.when(t > 0)
+            def _():
+                inner(i, size, base_chunk).wait_recv()
+
+            step(first_z + i * size, size)
+            return carry
+
+        lax.fori_loop(0, count, body, 0)
 
     def transformed(begin, count):
         slabs = []
@@ -354,7 +384,7 @@
             jnp.concatenate([slabs[x] + slabs[x + half], slabs[x] - slabs[x + half]], axis=1)
             for x in range(half)
         ]
-        turned = product(halves(jnp.concatenate(pairs, axis=0)), (ytab[0], ytab[1]), ((1,), (0,)))
+        turned = product(halves(jnp.concatenate(pairs, axis=0)), (ytab(0), ytab(1)), ((1,), (0,)))
         parts = [turned[x * 3 * count:(x + 1) * 3 * count] for x in range(half)]
         mixed = []
         for j in range(half):
@@ -386,7 +416,7 @@
         def go(a, to_t, to_s):
             remote(
                 source_of(pl.ds(pl.multiple_of(a * 8, 8), 8)), target.at[slot],
-                sems.at[sem], sems.at[sem + 1], (to_t, to_s),
+                sems.at[0], sems.at[sem], (to_t, to_s),
             ).start()
 
         if paired:
@@ -415,9 +445,8 @@
             )
         send_l[k] = jnp.transpose(staged[k])
 
-    early_steps = early_c * 2 // BLOCK
     with jax.named_scope("steps"):
-        lax.fori_loop(0, early_steps, main_step, 0)
+        main_steps(doubles, 2 * BLOCK, 0)
 
     with jax.named_scope("fwd_a"):
         for copy in tables:
@@ -435,16 +464,16 @@
     hear(rounds - 1)
     if early_c > 0:
         with jax.named_scope("issue_a"):
-            spread(lambda r: send_a.at[:, r], recv_a, 0)
+            spread(lambda r: send_a.at[:, r], recv_a, 1)
 
     with jax.named_scope("steps_m"):
-        lax.fori_loop(early_steps, steps, main_step, 0)
+        main_steps(singles, BLOCK, doubles)
 
     if middles:
         with jax.named_scope("fwd_m"):
             late(0)
         with jax.named_scope("issue_m"):
-            spread(lambda r: send_l.at[0, r], recv_l.at[0], 8)
+            spread(lambda r: send_l.at[0, r], recv_l.at[0], 6)
 
     with jax.named_scope("w_final"):
         @pl.when(t > 0)
@@ -457,19 +486,16 @@
     with jax.named_scope("fwd_b"):
         late(middles)
     with jax.named_scope("issue_b"):
-        spread(lambda r: send_l.at[middles, r], recv_l.at[middles], 6)
+        spread(lambda r: send_l.at[middles, r], recv_l.at[middles], 7)
 
     with jax.named_scope("sent"):
-        for copy in halos:
-            copy.wait_send()
-
         @pl.when(t < nt - 1)
         def _():
-            for copy in starts:
-                copy.wait_send()
-
-        for copy in inits:
-            copy.wait_send()
+            planes_wait(12 * HALO + depth, early_send)
+
+        @pl.when(t == nt - 1)
+        def _():
+            planes_wait(12 * HALO, early_send)
 
     def when_solver(body):
         if all_solve:
@@ -483,11 +509,9 @@
             pltpu.make_async_copy(part, part, sem).wait()
 
     def forward_sent(count):
-        if early_c > 0:
-            bytes_wait(recv_a, count, sems.at[0])
-        if middles:
-            bytes_wait(recv_l.at[0], count, sems.at[8])
-        bytes_wait(recv_l.at[middles], count, sems.at[6])
+        units = count * ((tiles if early_c > 0 else 0) + middles + 1)
+        part = restricted.at[pl.ds(0, 8 * units)]
+        pltpu.make_async_copy(part, part, sems.at[0]).wait()
 
     def carry_copy(to_t):
         return remote(carry_out, carry_in, sems.at[4], sems.at[5], (to_t, s))
@@ -522,7 +546,7 @@
                             chosen = jnp.where(lane == g, value, chosen)
                         columns.append(chosen)
                     fields.append(jnp.concatenate(columns, axis=1))
-                spectra = product(halves(jnp.concatenate(fields, axis=0)), (zearly[0], zearly[1]), ((1,), (0,)))
+                spectra = product(halves(jnp.concatenate(fields, axis=0)), (zearly(0), zearly(1)), ((1,), (0,)))
 
         def late_part(k):
             high = half * late_c
@@ -539,11 +563,11 @@
                         chosen = pltpu.roll(chosen, length - high * f, 1)
                     columns.append(chosen)
                 fields.append(jnp.concatenate(columns, axis=1))
-            return product(halves(jnp.concatenate(fields, axis=0)), (zlate[k, 0], zlate[k, 1]), ((1,), (0,)))
+            return product(halves(jnp.concatenate(fields, axis=0)), (zlate(k, 0), zlate(k, 1)), ((1,), (0,)))
 
         if middles:
             with jax.named_scope("w_recv_m"):
-                bytes_wait(recv_l.at[0], span * ns - 1, sems.at[9])
+                bytes_wait(recv_l.at[0], span * ns - 1, sems.at[6])
             with jax.named_scope("z_m"):
                 more = late_part(0)
                 spectra = more if spectra is None else spectra + more
@@ -583,7 +607,6 @@
                 def _():
                     carry_copy(t + span).start()
 
-            whole_c = zback.shape[1] // 2
             rows_all = jnp.concatenate(
                 [
                     jnp.concatenate([value[:, j * whole_c:(j + 1) * whole_c] for field in fields for value in field], axis=0)
@@ -593,7 +616,7 @@
             )
             upper, lower = halves(rows_all)
             wide = lax.dot_general(
-                jnp.concatenate([upper, lower], axis=1), zback[...], (((1,), (0,)), ((), ())),
+                jnp.concatenate([upper, lower], axis=1), zback(), (((1,), (0,)), ((), ())),
                 preferred_element_type=jnp.float32,
             )
             back = wide[:, :whole_c] + wide[:, whole_c:]
@@ -651,7 +674,7 @@
     when_solver(sent)
 
 
-def finish(w, recv, ytab, xtab, out, returned, up, result, sems):
+def finish(w, recv, half_tab, full_tab, out, returned, up, result, sems):
     _, _, interp = node_tables()
     depth, rows, cols = out.shape[2:]
     depth_c, rows_c = depth // 2, rows // 2
@@ -660,6 +683,9 @@
     count = depth_c // up.shape[0]
     s = lax.axis_index("space")
     slabs = length // depth_c
+    width = solvers * 8
+    _, ytab, _, _, _ = tables_of(half_tab, width, length, 0, 0)
+    xtab = full_tab.at[pl.ds(width, half * half), pl.ds(0, width)]
     for f in range(3):
         returned[f] = jnp.transpose(recv[:, f].reshape(solvers * 8, length))
     places = [lax.rem(s + j, slabs) * depth_c for j in range(half)]
@@ -681,7 +707,7 @@
                 term = xtab[pl.ds(j * half + x, 1), :] * mixed[j]
                 total = term if total is None else total + term
             parts.append(total)
-        coarse = product(halves(jnp.concatenate(parts, axis=0)), (ytab[0], ytab[1]), ((1,), (1,)))
+        coarse = product(halves(jnp.concatenate(parts, axis=0)), (ytab(0), ytab(1)), ((1,), (1,)))
         high = 3 * count
         for x in range(rows_c):
             part = coarse[(x % half) * high:(x % half + 1) * high, (x // half) * cols:(x // half + 1) * cols]
@@ -738,7 +764,7 @@
     early_c = depth_c - (1 + middles) * late_c
     per_tile = length // (half * early_c) if early_c else 1
     tiles = -(-3 // per_tile) if early_c else 1
-    early_sets = -(-ns // per_tile)
+    early_sets = -(-ns // per_tile) if early_c else 0
     zearly = np.zeros((early_sets, length, half * whole_c))
     zlate = np.zeros((middles + 1, sets * blocks, half, late_c, half, whole_c))
     for j in range(half):
@@ -749,8 +775,6 @@
             begin = early_c + k * late_c
             zlate[k, :ns, j, :, j] = wave_z[:, begin:begin + late_c]
     zearly = two_parts(zearly.reshape(early_sets * length, half * whole_c))
-    if early_c == 0:
-        zearly = zearly[:, :16]
     zlate = np.stack([two_parts(part.reshape(sets * length, half * whole_c)) for part in zlate])
     wave = two_parts(hartley(whole_c))
     zback = np.block([[wave[0], wave[1]], [wave[0], np.zeros_like(wave[0])]])
@@ -763,16 +787,24 @@
     inv = (1.0 / (1.0 - 0.5 * step_length * diffusion * eigen)).astype(np.float32)
     inv = inv.reshape(width, half * whole_c)
 
+    total = half * whole_c
+    misc = np.zeros((4 * width, total), jnp.bfloat16)
+    misc[:, :width] = ytab[0].reshape(4 * width, width)
+    misc[:, width:2 * width] = ytab[1].reshape(4 * width, width)
+    misc[:2 * whole_c, 2 * width:2 * width + 2 * whole_c] = zback
+    half_tab = np.concatenate([misc, zearly.reshape(-1, total), zlate.reshape(-1, total)], axis=0)
+    full_tab = np.zeros((width + half * half, total), np.float32)
+    full_tab[:width], full_tab[width:, :width] = inv, xtab
     f32 = jnp.float32
     bf16 = jnp.bfloat16
-    arrays = (u_old, u_init, ytab, xtab, zback, zearly, zlate, inv)
+    arrays = (u_old, u_init, half_tab, full_tab)
     handed = pl.pallas_call(
         functools.partial(kernel, nt, ns, groups),
         out_shape=(
             jax.ShapeDtypeStruct((5, extended, rows, cols), f32),
             jax.ShapeDtypeStruct((solvers, 3, 8, length), f32),
-            jax.ShapeDtypeStruct(ytab.shape[1:], bf16),
-            jax.ShapeDtypeStruct(xtab.shape, f32),
+            jax.ShapeDtypeStruct(half_tab.shape, bf16),
+            jax.ShapeDtypeStruct(full_tab.shape, f32),
         ),
         in_specs=[pl.BlockSpec(memory_space=pltpu.HBM)] * len(arrays),
         out_specs=(pl.BlockSpec(memory_space=pltpu.VMEM),) * 4,
@@ -781,11 +813,6 @@
             pltpu.VMEM((4, extended, rows, cols), f32),
             pltpu.VMEM((4, extended, rows, cols), f32),
             pltpu.VMEM((3 * depth_c * rows, cols), f32),
-            pltpu.VMEM(ytab.shape[1:], bf16),
-            pltpu.VMEM(zback.shape, bf16),
-            pltpu.VMEM(zearly.shape, bf16),
-            pltpu.VMEM(zlate.shape, bf16),
-            pltpu.VMEM(inv.shape, f32),
             pltpu.VMEM((tiles, width, length), f32),
             pltpu.VMEM((span * ns, tiles, 8, length), f32),
             pltpu.VMEM((middles + 1, length, width), f32),
@@ -795,13 +822,12 @@
             pltpu.VMEM((8, half * whole_c), f32),
             pltpu.VMEM((8, half * whole_c), f32),
             pltpu.SemaphoreType.DMA,
-            pltpu.SemaphoreType.DMA((7,)),
+            pltpu.SemaphoreType.DMA((2,)),
+            pltpu.SemaphoreType.DMA,
             pltpu.SemaphoreType.DMA,
             pltpu.SemaphoreType.DMA((2,)),
-            pltpu.SemaphoreType.DMA((2,)),
-            pltpu.SemaphoreType.DMA((5 + steps,)),
-            pltpu.SemaphoreType.DMA((5 + steps,)),
-            pltpu.SemaphoreType.DMA((10,)),
+            pltpu.SemaphoreType.DMA((steps - early_c // BLOCK + 1,)),
+            pltpu.SemaphoreType.DMA((8,)),
             pltpu.SemaphoreType.REGULAR((rounds,)),
         ],
         compiler_params=pltpu.CompilerParams(

time: 29.6 us -> 29.4 us (level)
  Pallas kernels: 29.5 us -> 29.2 us
where the time goes in v4:
time: 29.4 us; the launch traced here: 29.2 us
  Pallas kernels  29.2 us (99%)
    pallas_call x1, Pallas kernels, shards(): pl.pallas_call(functools.partial(kernel, nt, ns, groups), out_shape=(jax....  27.2 us
    pallas_call x1, Pallas kernels, shards(): pl.pallas_call(finish, out_shape=jax.ShapeDtypeStruct((1, 5, depth, rows,...  2.08 us

profile of v4, /device:TPU:17, one launch (start us, length us, event | category | flops | bytes accessed | tf_op | source)
XLA Modules:
  0.0 29.2 jit_solution(94432941682462534)
XLA Ops:
  0.0 27.2 %shard_map.46 = (f32[5,74,16,128]{3,2,1,0:T(8,128)S(1)}, f32[16,3,8,128]{3,2,1,0:T(8,128)S(1)}, bf16[1536,512]{1,0:T(8,128)(2,1)S(1)}, f32[144,512]{1,0:T(8,128)S(1)}) custom-call(f32[1,5,64,16,128]{4,3,2,1,0:T(8,128)} %u_hbm.1, f32[64,16,128]{2,1,0:T(8,128)} %init_hbm.1, bf16[1536,512]{1,0:T(8,128)(2,1)} %constant.4.clone.half_tab_hbm, ...), custom_call_target="tpu_custom_call" | custom-call | tf_op jit(solution)/shard_map/pallas_call | solution.py:801
  27.2 2.1 %shard_map.47 = f32[1,5,64,16,128]{4,3,2,1,0:T(8,128)} custom-call(f32[5,74,16,128]{3,2,1,0:T(8,128)S(1)} %get-tuple-element.9.w, f32[16,3,8,128]{3,2,1,0:T(8,128)S(1)} %get-tuple-element.10.recv, bf16[1536,512]{1,0:T(8,128)(2,1)S(1)} %get-tuple-element.11.half_tab, f32[144,512]{1,0:T(8,128)S(1)} %get-tuple-element.12.full_tab), custom_call_target="tpu_custom_call" | custom-call | tf_op jit(solution)/shard_map/pallas_call | solution.py:837

commit v5 on v4

--- a/solution.py
+++ b/solution.py
@@ -14,6 +14,8 @@
 reaction = 1.0
 HALO = 5
 BLOCK = 8
+AHEAD = 2
+RELAYS = 3
 GROUPS = 2
 MESH = pl.DeviceIdType.MESH
 
@@ -130,7 +132,8 @@
     w, recv_2, half_tab, full_tab,
     u, corr, forces, restricted,
     send_a, recv_a, staged, send_l, recv_l, send_2, carry_out, carry_in,
-    load_sem, table_sem, start_sem, early_send, edge_recv, start_recv,
+    held,
+    load_sem, table_sem, start_sem, early_send, edge_recv, start_recv, relay_sems,
     sems, known_sem,
 ):
     integ, spacing, _ = node_tables()
@@ -214,7 +217,15 @@
     node = u_hbm.at[0, 4]
     steps = depth // BLOCK - 2
     doubles = early_c // BLOCK
-    singles = steps - 2 * doubles
+    chunks = [(HALO + i * 2 * BLOCK, 2 * BLOCK) for i in range(doubles - 1)]
+    singles = steps - 2 * len(chunks)
+    chunks += [(HALO + (steps - singles + i) * BLOCK, BLOCK) for i in range(singles)]
+    chunks.append((HALO + steps * BLOCK, depth - 2 * HALO - steps * BLOCK))
+    relays = min(held.shape[0], max(0, singles - 1)) if nt > 4 else 0
+    relayed = len(chunks) - 1 - relays
+
+    def relays_of(to):
+        return jnp.where(to == 1, relays, 0)
 
     def start_piece(sem, begin, size):
         return remote(
@@ -222,8 +233,8 @@
             early_send, sem, (after, s),
         )
 
-    def inner(i, size, base_chunk):
-        return start_piece(start_recv.at[base_chunk + i], HALO + (2 * doubles if base_chunk else 0) * BLOCK + i * size, size)
+    def chunk(i):
+        return start_piece(start_recv.at[i], *chunks[i])
 
     def planes_wait(count, sem):
         whole = next(k for k in range(1, 6) if count % k == 0 and count // k <= extended)
@@ -231,9 +242,6 @@
         pltpu.make_async_copy(part, part, sem).wait()
 
     start_edges = [start_piece(edge_recv.at[0], 0, HALO), start_piece(edge_recv.at[0], depth - HALO, HALO)]
-    final = start_piece(start_recv.at[doubles + singles], HALO + steps * BLOCK, depth - 2 * HALO - steps * BLOCK)
-    starts = start_edges + [inner(i, 2 * BLOCK, 0) for i in range(doubles)]
-    starts += [inner(i, BLOCK, doubles) for i in range(singles)] + [final]
 
     def edges(source, shift):
         return [
@@ -253,10 +261,27 @@
         remote(u_hbm.at[0, :, first], u.at[:, highs], early_send, load_sem, (t, below)),
     ]
 
+    mine_relayed, theirs_relayed = relays_of(t), relays_of(t + 1)
+
     @pl.when(t < nt - 1)
     def _():
-        for copy in starts:
+        for copy in start_edges:
             copy.start()
+        for i in range(len(chunks)):
+            k = i - relayed
+            if 0 <= k < relays:
+                @pl.when(mine_relayed >= relays - k)
+                def _(i=i, k=k):
+                    begin, size = chunks[i]
+                    remote(
+                        node.at[pl.ds(begin, size)], held.at[k], early_send, relay_sems.at[0], (t - 1, s)
+                    ).start()
+
+                @pl.when(mine_relayed < relays - k)
+                def _(i=i):
+                    chunk(i).start()
+            else:
+                chunk(i).start()
 
     for copy in halos:
         copy.start()
@@ -289,6 +314,16 @@
 
     if rounds > 2:
         hear(1)
+    for count in range(1, relays + 1):
+        @pl.when(theirs_relayed == count)
+        def _(count=count):
+            planes_wait(count * BLOCK, relay_sems.at[0])
+            for k in range(relays - count, relays):
+                begin, size = chunks[relayed + k]
+                remote(
+                    held.at[k], w.at[0, pl.ds(HALO + begin, size)], relay_sems.at[1],
+                    start_recv.at[relayed + k], (t + 2, s),
+                ).start()
 
     def fold_block(i, carry):
         z = 1 + i * BLOCK
@@ -357,18 +392,14 @@
             count = BLOCK - 2 * m
             advance(m, w[m, pl.ds(m, count + 2)], pl.ds(1 + m, count))
 
-    def main_steps(count, size, base_chunk):
-        first_z = HALO + 4 + (2 * doubles if base_chunk else 0) * BLOCK
-
-        def body(i, carry):
-            @pl.when(t > 0)
-            def _():
-                inner(i, size, base_chunk).wait_recv()
-
-            step(first_z + i * size, size)
-            return carry
-
-        lax.fori_loop(0, count, body, 0)
+    def main_step(begin, size):
+        @pl.when(t > 0)
+        def _():
+            for i, (first_z, count) in enumerate(chunks):
+                if begin <= first_z and first_z + count <= begin + size:
+                    chunk(i).wait_recv()
+
+        step(begin + 4, size)
 
     def transformed(begin, count):
         slabs = []
@@ -446,7 +477,8 @@
         send_l[k] = jnp.transpose(staged[k])
 
     with jax.named_scope("steps"):
-        main_steps(doubles, 2 * BLOCK, 0)
+        for i in range(doubles):
+            main_step(HALO + i * 2 * BLOCK, 2 * BLOCK)
 
     with jax.named_scope("fwd_a"):
         for copy in tables:
@@ -462,23 +494,29 @@
                 send_a[i] = jnp.transpose(jnp.concatenate(parts, axis=0))
 
     hear(rounds - 1)
+    def issue_early():
+        spread(lambda r: send_a.at[:, r], recv_a, 1)
+
     if early_c > 0:
         with jax.named_scope("issue_a"):
-            spread(lambda r: send_a.at[:, r], recv_a, 1)
+            pl.when(t > 0)(issue_early)
 
     with jax.named_scope("steps_m"):
-        main_steps(singles, BLOCK, doubles)
+        for i in range(2 * doubles, steps):
+            main_step(HALO + i * BLOCK, BLOCK)
 
     if middles:
         with jax.named_scope("fwd_m"):
             late(0)
+        if early_c > 0:
+            pl.when(t == 0)(issue_early)
         with jax.named_scope("issue_m"):
             spread(lambda r: send_l.at[0, r], recv_l.at[0], 6)
 
     with jax.named_scope("w_final"):
         @pl.when(t > 0)
         def _():
-            final.wait_recv()
+            chunk(len(chunks) - 1).wait_recv()
 
     with jax.named_scope("tail"):
         step(HALO + 4 + steps * BLOCK, 2 * BLOCK)
@@ -496,6 +534,11 @@
         @pl.when(t == nt - 1)
         def _():
             planes_wait(12 * HALO, early_send)
+
+        for count in range(1, relays + 1):
+            @pl.when(theirs_relayed == count)
+            def _(count=count):
+                planes_wait(count * BLOCK, relay_sems.at[1])
 
     def when_solver(body):
         if all_solve:
@@ -693,7 +736,7 @@
     def give(p):
         return pltpu.make_async_copy(result.at[p], out.at[0, :, pl.ds(p * 2 * count, 2 * count)], sems.at[p])
 
-    for p in range(up.shape[0]):
+    def spread_up(p):
         mixed = [
             jnp.concatenate(
                 [returned[f, pl.ds(pl.multiple_of(places[j] + p * count, 8), count), :] for f in range(3)], axis=0
@@ -713,6 +756,8 @@
             part = coarse[(x % half) * high:(x % half + 1) * high, (x // half) * cols:(x // half + 1) * cols]
             for side in range(2):
                 up[p, pl.ds(2 * x + side, high, stride=rows), :] = part
+
+    def add(p):
         for z in range(count):
             fields = [up[p, pl.ds((f * count + z) * rows, rows), :] for f in range(3)]
             for m in range(5):
@@ -727,6 +772,15 @@
                 for side in range(2):
                     result[p, m, 2 * z + side] = w[m, HALO + 2 * (p * count + z) + side] + total
         give(p).start()
+
+    parts = up.shape[0]
+    ahead = min(AHEAD, parts)
+    for p in range(ahead):
+        spread_up(p)
+    for p in range(parts):
+        if p + ahead < parts:
+            spread_up(p + ahead)
+        add(p)
     for p in range(up.shape[0]):
         give(p).wait()
 
@@ -821,12 +875,14 @@
             pltpu.VMEM((span * ns, 3, 8, length), f32),
             pltpu.VMEM((8, half * whole_c), f32),
             pltpu.VMEM((8, half * whole_c), f32),
+            pltpu.VMEM((RELAYS, BLOCK, rows, cols), f32),
             pltpu.SemaphoreType.DMA,
             pltpu.SemaphoreType.DMA((2,)),
             pltpu.SemaphoreType.DMA,
             pltpu.SemaphoreType.DMA,
             pltpu.SemaphoreType.DMA((2,)),
-            pltpu.SemaphoreType.DMA((steps - early_c // BLOCK + 1,)),
+            pltpu.SemaphoreType.DMA((steps - max(0, early_c // BLOCK - 1) + 1,)),
+            pltpu.SemaphoreType.DMA((2,)),
             pltpu.SemaphoreType.DMA((8,)),
             pltpu.SemaphoreType.REGULAR((rounds,)),
         ],

time: 29.4 us -> 29.1 us (0.990)
  no operation moved by 1% of the time
where the time goes in v5:
time: 29.1 us; the launch traced here: 29 us
  Pallas kernels  29 us (100%)
    pallas_call x1, Pallas kernels, shards(): pl.pallas_call(functools.partial(kernel, nt, ns, groups), out_shape=(jax....  26.9 us
    pallas_call x1, Pallas kernels, shards(): pl.pallas_call(finish, out_shape=jax.ShapeDtypeStruct((1, 5, depth, rows,...  2.08 us

profile of v5, /device:TPU:17, one launch (start us, length us, event | category | flops | bytes accessed | tf_op | source)
XLA Modules:
  0.0 29.0 jit_solution(3105655592766384922)
XLA Ops:
  0.0 26.9 %shard_map.46 = (f32[5,74,16,128]{3,2,1,0:T(8,128)S(1)}, f32[16,3,8,128]{3,2,1,0:T(8,128)S(1)}, bf16[1536,512]{1,0:T(8,128)(2,1)S(1)}, f32[144,512]{1,0:T(8,128)S(1)}) custom-call(f32[1,5,64,16,128]{4,3,2,1,0:T(8,128)} %u_hbm.1, f32[64,16,128]{2,1,0:T(8,128)} %init_hbm.1, bf16[1536,512]{1,0:T(8,128)(2,1)} %constant.4.clone.half_tab_hbm, ...), custom_call_target="tpu_custom_call" | custom-call | tf_op jit(solution)/shard_map/pallas_call | solution.py:855
  26.9 2.1 %shard_map.47 = f32[1,5,64,16,128]{4,3,2,1,0:T(8,128)} custom-call(f32[5,74,16,128]{3,2,1,0:T(8,128)S(1)} %get-tuple-element.9.w, f32[16,3,8,128]{3,2,1,0:T(8,128)S(1)} %get-tuple-element.10.recv, bf16[1536,512]{1,0:T(8,128)(2,1)S(1)} %get-tuple-element.11.half_tab, f32[144,512]{1,0:T(8,128)S(1)} %get-tuple-element.12.full_tab), custom_call_target="tpu_custom_call" | custom-call | tf_op jit(solution)/shard_map/pallas_call | solution.py:893

commit v6 on v5

--- a/solution.py
+++ b/solution.py
@@ -113,7 +113,7 @@
 
 def far_first(flip):
     hops = bin(flip[0]).count("1") + bin(flip[1] // 2).count("1")
-    return -(flip[1] // 2), -hops, -flip[0]
+    return -(flip[1] // 2), -hops, flip
 
 
 def force(padded):

time: 29.1 us -> 29.1 us (level)
  no operation moved by 1% of the time
where the time goes in v6:
time: 29.1 us; the launch traced here: 29 us
  Pallas kernels  29 us (100%)
    pallas_call x1, Pallas kernels, shards(): pl.pallas_call(functools.partial(kernel, nt, ns, groups), out_shape=(jax....  26.9 us
    pallas_call x1, Pallas kernels, shards(): pl.pallas_call(finish, out_shape=jax.ShapeDtypeStruct((1, 5, depth, rows,...  2.08 us

profile of v6, /device:TPU:17, one launch (start us, length us, event | category | flops | bytes accessed | tf_op | source)
XLA Modules:
  0.0 29.0 jit_solution(1839778283870122350)
XLA Ops:
  0.0 26.9 %shard_map.46 = (f32[5,74,16,128]{3,2,1,0:T(8,128)S(1)}, f32[16,3,8,128]{3,2,1,0:T(8,128)S(1)}, bf16[1536,512]{1,0:T(8,128)(2,1)S(1)}, f32[144,512]{1,0:T(8,128)S(1)}) custom-call(f32[1,5,64,16,128]{4,3,2,1,0:T(8,128)} %u_hbm.1, f32[64,16,128]{2,1,0:T(8,128)} %init_hbm.1, bf16[1536,512]{1,0:T(8,128)(2,1)} %constant.4.clone.half_tab_hbm, ...), custom_call_target="tpu_custom_call" | custom-call | tf_op jit(solution)/shard_map/pallas_call | solution.py:855
  26.9 2.1 %shard_map.47 = f32[1,5,64,16,128]{4,3,2,1,0:T(8,128)} custom-call(f32[5,74,16,128]{3,2,1,0:T(8,128)S(1)} %get-tuple-element.9.w, f32[16,3,8,128]{3,2,1,0:T(8,128)S(1)} %get-tuple-element.10.recv, bf16[1536,512]{1,0:T(8,128)(2,1)S(1)} %get-tuple-element.11.half_tab, f32[144,512]{1,0:T(8,128)S(1)} %get-tuple-element.12.full_tab), custom_call_target="tpu_custom_call" | custom-call | tf_op jit(solution)/shard_map/pallas_call | solution.py:893
